TPU v7x, 32 devices: a whole 2x2x4 slice. The times are simulated.
32 devices in a mesh: wide: 8 (over z, x), narrow: 4 (over y, core).
Axes of the slice: x: 2, y: 2, z: 4, core: 2. Of those that a mesh axis runs over, the one named last changes fastest.
Arguments:
- rows: bfloat16 [8192, 1024], P(('wide', 'narrow')), may hold values from -6 to 6
- grades: int32 [8192], P(('wide', 'narrow')), may hold values from 0 to 4
- block_dest: int32 [32, 8], P(('wide', 'narrow')), may hold values from 0 to 7, each once within a row
- block_source: int32 [32, 8], P(('wide', 'narrow')), may hold values from 0 to 7, each once within a row
- lengths: int32 [8, 3], replicated, may hold values from 1 to 640, 1024 in all within a row
- gain: float32 [1024], replicated, may hold values from 0.5 to 1.5
- w_qkv: bfloat16 [1024, 3072], replicated, may hold values from -0.1875 to 0.1875
- w_out: bfloat16 [1024, 1024], replicated, may hold values from -0.1875 to 0.1875
- w_score: float32 [1024], replicated, may hold values from -0.1875 to 0.1875
Outputs:
- grad_rows: bfloat16 [8192, 1024], P(('wide', 'narrow'))
- grad_qkv: float32 [1024, 3072], P(None, ('wide', 'narrow'))
- grad_out: float32 [1024, 1024], P(None, ('wide', 'narrow'))
Inputs may be any that keep to these rules, and one draw needn't show every extreme that they name: Each row of block_dest and of block_source names every group once. The lengths of one group sum to 1024.
All inputs are finite; a program needn't handle non-finite values.
Results may differ from a plain program's by a relative error of at most 0.0095.
Values may be sent and summed in bfloat16 or wider, within the bound.
No kernel may reach another device: no remote copies, remote signals or barrier semaphores. Data moves between devices by JAX's collectives and lax.ppermute only.
A program may use at most 128 MiB of HBM per device.

v0:
```python
import jax
import jax.numpy as jnp
from jax import lax
from jax.sharding import PartitionSpec as P

HEADS = 16


epsilon = 1e-06
loss_scale = 64.0
block_heads = 2


def to_blocks(values, count, head_size):
    return values.reshape(count, HEADS // block_heads, block_heads, head_size).transpose(1, 2, 0, 3)


def from_blocks(values, count, width):
    return values.transpose(2, 0, 1, 3).reshape(count, width)


def body(rows, grades, block_dest, block_source, lengths, gain, w_qkv, w_out, w_score):
    wide_count = lax.axis_size("wide")
    narrow_count = lax.axis_size("narrow")
    local_rows, width = rows.shape
    piece = local_rows // wide_count
    head_size = width // HEADS
    scale = head_size ** (-0.5)
    group_total = local_rows * narrow_count
    slots = jnp.arange(wide_count, dtype=jnp.int32)
    dest = block_dest[0]
    source = block_source[0]
    dest_inverse = jnp.sum(
        slots[None, :] * (dest[None, :] == slots[:, None]).astype(jnp.int32), axis=1
    )
    source_inverse = jnp.sum(
        slots[None, :] * (source[None, :] == slots[:, None]).astype(jnp.int32), axis=1
    )
    outgoing = rows.reshape(wide_count, piece, width)[dest_inverse]
    grade_out = grades.astype(jnp.bfloat16).reshape(wide_count, piece)[dest_inverse]
    incoming, grade_in = (
        lax.all_to_all(outgoing, "wide", split_axis=0, concat_axis=0, tiled=True),
        lax.all_to_all(grade_out, "wide", split_axis=0, concat_axis=0, tiled=True),
    )
    work = incoming[source].reshape(local_rows, width)
    work_grades = grade_in[source].reshape(local_rows)
    group_index = lax.axis_index("wide")
    narrow_index = lax.axis_index("narrow")
    group_lengths = lax.dynamic_index_in_dim(lengths, group_index, 0, keepdims=False)
    bounds = jnp.cumsum(group_lengths)
    positions = jnp.arange(group_total, dtype=jnp.int32)
    segment_all = jnp.sum((positions[:, None] >= bounds[None, :]).astype(jnp.int32), axis=1)
    segment_own = lax.dynamic_slice_in_dim(segment_all, narrow_index * local_rows, local_rows)
    same = (segment_own[:, None] == segment_all[None, :]).astype(jnp.float32)
    rows_f32 = work.astype(jnp.float32)
    inverse = lax.rsqrt(jnp.mean(rows_f32 * rows_f32, axis=1) + epsilon)
    normed = (rows_f32 * inverse[:, None] * gain).astype(jnp.bfloat16)
    projected = jnp.dot(normed, w_qkv, preferred_element_type=jnp.float32).astype(jnp.bfloat16)
    key_value = lax.all_gather(projected[:, width:], "narrow", axis=0, tiled=True)
    query_blocks = to_blocks(projected[:, :width], local_rows, head_size)
    key_blocks = to_blocks(key_value[:, :width], group_total, head_size)
    value_blocks = to_blocks(key_value[:, width:], group_total, head_size)

    def attend_probs(query_part, key_part, mask):
        logits = (
            jnp.einsum("hqd,hkd->hqk", query_part, key_part, preferred_element_type=jnp.float32)
            * scale
        )
        return jnp.exp(logits) * mask[None]

    def forward_block(inputs):
        query_part, key_part, value_part = inputs
        weights = attend_probs(query_part, key_part, same)
        totals = jnp.sum(weights, axis=2)
        probs_bf = (weights / totals[:, :, None]).astype(jnp.bfloat16)
        attended_part = jnp.einsum(
            "hqk,hkd->hqd", probs_bf, value_part, preferred_element_type=jnp.float32
        )
        return (attended_part, totals)

    attended_blocks, totals_blocks = lax.map(
        forward_block, (query_blocks, key_blocks, value_blocks)
    )
    attended = from_blocks(attended_blocks, local_rows, width).astype(jnp.bfloat16)
    hidden = rows_f32 + jnp.dot(attended, w_out, preferred_element_type=jnp.float32)
    scores = jnp.dot(hidden, w_score, precision=lax.Precision.HIGHEST)
    gains = jnp.exp2(work_grades.astype(jnp.float32))
    scores_all, gains_all = (
        lax.all_gather(scores, "narrow", axis=0, tiled=True),
        lax.all_gather(gains, "narrow", axis=0, tiled=True),
    )
    norm_sum = jnp.dot(same, gains_all, precision=lax.Precision.HIGHEST)
    spread = gains[:, None] - gains_all[None, :]
    margins = scores[:, None] - scores_all[None, :]
    upper = jnp.maximum(spread, 0.0) * same
    lower = jnp.maximum(-spread, 0.0) * same
    score_grad = (
        loss_scale
        * jnp.sum(lower * jax.nn.sigmoid(margins) - upper * jax.nn.sigmoid(-margins), axis=1)
        / norm_sum
    )
    hidden_grad = score_grad[:, None] * w_score[None, :]
    hidden_bf = hidden_grad.astype(jnp.bfloat16)
    out_part = jnp.einsum("rd,re->de", attended, hidden_bf, preferred_element_type=jnp.float32)
    upstream_flat = jnp.einsum(
        "re,de->rd", hidden_bf, w_out, preferred_element_type=jnp.float32
    ).astype(jnp.bfloat16)
    upstream_blocks = to_blocks(upstream_flat, local_rows, head_size)
    attended_heads = to_blocks(attended, local_rows, head_size)
    delta_blocks = jnp.sum(
        upstream_blocks.astype(jnp.float32) * attended_heads.astype(jnp.float32), axis=3
    )

    def backward_block(inputs):
        query_part, key_part, value_part, upstream_part, totals, delta = inputs
        probs = attend_probs(query_part, key_part, same) / totals[:, :, None]
        prob_grad = jnp.einsum(
            "hqd,hkd->hqk", upstream_part, value_part, preferred_element_type=jnp.float32
        )
        logit_grad = (probs * (prob_grad - delta[:, :, None]) * scale).astype(jnp.bfloat16)
        query_grad = jnp.einsum(
            "hqk,hkd->hqd", logit_grad, key_part, preferred_element_type=jnp.float32
        )
        return query_grad

    back_inputs = (
        query_blocks,
        key_blocks,
        value_blocks,
        upstream_blocks,
        totals_blocks,
        delta_blocks,
    )
    query_grad = from_blocks(lax.map(backward_block, back_inputs), local_rows, width)
    query_all, upstream_all = (
        lax.all_gather(projected[:, :width], "narrow", axis=0, tiled=True),
        lax.all_gather(upstream_flat, "narrow", axis=0, tiled=True),
    )
    totals_all, delta_all = (
        lax.all_gather(totals_blocks.astype(jnp.bfloat16), "narrow", axis=2, tiled=True).astype(
            totals_blocks.dtype
        ),
        lax.all_gather(delta_blocks.astype(jnp.bfloat16), "narrow", axis=2, tiled=True).astype(
            delta_blocks.dtype
        ),
    )
    query_all_blocks = to_blocks(query_all, group_total, head_size)
    upstream_all_blocks = to_blocks(upstream_all, group_total, head_size)
    key_own = to_blocks(projected[:, width : 2 * width], local_rows, head_size)
    value_own = to_blocks(projected[:, 2 * width :], local_rows, head_size)
    same_back = same.T

    def reverse_block(inputs):
        query_part, key_part, value_part, upstream_part, totals, delta = inputs
        probs_back = attend_probs(query_part, key_part, same_back) / totals[:, :, None]
        grad_back = jnp.einsum(
            "hqd,hkd->hqk", upstream_part, value_part, preferred_element_type=jnp.float32
        )
        logit_back = (probs_back * (grad_back - delta[:, :, None]) * scale).astype(jnp.bfloat16)
        key_grad = jnp.einsum(
            "hqk,hqd->hkd", logit_back, query_part, preferred_element_type=jnp.float32
        )
        value_grad = jnp.einsum(
            "hqk,hqd->hkd",
            probs_back.astype(jnp.bfloat16),
            upstream_part,
            preferred_element_type=jnp.float32,
        )
        return (key_grad, value_grad)

    key_blocks_own, value_blocks_own = lax.map(
        reverse_block,
        (query_all_blocks, key_own, value_own, upstream_all_blocks, totals_all, delta_all),
    )
    key_grad = from_blocks(key_blocks_own, local_rows, width)
    value_grad = from_blocks(value_blocks_own, local_rows, width)
    proj_grad = jnp.concatenate([query_grad, key_grad, value_grad], axis=1).astype(jnp.bfloat16)
    qkv_part = jnp.einsum("rd,re->de", normed, proj_grad, preferred_element_type=jnp.float32)
    normed_grad = jnp.einsum("re,de->rd", proj_grad, w_qkv, preferred_element_type=jnp.float32)
    scaled = normed_grad * gain
    row_grad = (
        hidden_grad
        + inverse[:, None] * scaled
        - rows_f32 * (inverse**3)[:, None] * jnp.mean(scaled * rows_f32, axis=1)[:, None]
    )
    row_grad_bf = row_grad.astype(jnp.bfloat16)
    returning = row_grad_bf.reshape(wide_count, piece, width)[source_inverse]
    arrived = lax.all_to_all(returning, "wide", split_axis=0, concat_axis=0, tiled=True)
    grad_rows = arrived[dest].reshape(local_rows, width)
    grad_qkv, grad_out = (
        lax.psum_scatter(qkv_part, ("wide", "narrow"), scatter_dimension=1, tiled=True),
        lax.psum_scatter(out_part, ("wide", "narrow"), scatter_dimension=1, tiled=True),
    )
    return (grad_rows, grad_qkv, grad_out)


def solution(mesh):
    placed = (
        P(("wide", "narrow"), None),
        P(("wide", "narrow")),
        P(("wide", "narrow"), None),
        P(("wide", "narrow"), None),
        P(),
        P(),
        P(),
        P(),
        P(),
    )
    return jax.shard_map(
        body,
        mesh=mesh,
        in_specs=placed,
        out_specs=(
            P(("wide", "narrow"), None),
            P(None, ("wide", "narrow")),
            P(None, ("wide", "narrow")),
        ),
        check_vma=False,
    )
```

profile of v0, /device:TPU:0, one launch (start us, length us, event | category | flops | bytes accessed | tf_op | source)
XLA Modules:
  0.0 507.3 jit_solution(10741471312392354073)
XLA Ops:
  8.1 2.4 gather_fusion.2
  10.6 7.3 %all-to-all-start.1 = ((bf16[8,32,1024]{2,1,0:T(8,128)(2,1)}), bf16[8,32,1024]{2,1,0:T(8,128)(2,1)S(1)}, u32[]{:S(2)}, u32[]{:S(2)}) async-start(bf16[8,32,1024]{2,1,0:T(8,128)(2,1)} %gather_fusion.2), calls=%async_computation.1 | async-start | bytes 1048576 | tf_op jit(solution)/shard_map/all_to_all | solution.py:42
  17.9 14.4 %all-to-all-done.1 = bf16[8,32,1024]{2,1,0:T(8,128)(2,1)S(1)} async-done(((bf16[8,32,1024]{2,1,0:T(8,128)(2,1)}), bf16[8,32,1024]{2,1,0:T(8,128)(2,1)S(1)}, u32[]{:S(2)}, u32[]{:S(2)}) %all-to-all-start.1) | async-done | bytes 524320 | tf_op jit(solution)/shard_map/all_to_all | solution.py:42
  33.4 4.8 convolution_convert_fusion
  40.7 2.5 slice.38
  44.4 3.6 all-to-all-start
  48.7 5.8 %all-to-all-done = bf16[8,1,32]{2,1,0:T(2,128)(2,1)S(1)} async-done(((bf16[8,1,32]{2,1,0:T(2,128)(2,1)}), bf16[8,1,32]{2,1,0:T(2,128)(2,1)S(1)}, u32[]{:S(2)}, u32[]{:S(2)}) %all-to-all-start) | async-done | bytes 544 | tf_op jit(solution)/shard_map/all_to_all | solution.py:43
  55.2 5.2 %all-gather = f32[4,1,256]{2,1,0:T(1,128)S(1)} all-gather(f32[1,1,256]{2,1,0:T(1,128)S(1)} %reshape.289), channel_id=1, replica_groups=mesh['wide'=8,'narrow'=4] {'narrow'}, dimensions={0}, use_global_device_ids=true | all-gather | bytes 5120 | tf_op jit(solution)/shard_map/all_gather | solution.py:90
  62.0 2.0 copy.59
  64.1 2.0 copy.61
  66.1 3.9 copy.58
  70.1 28.4 %all-gather.6.cloned.1.call-done = bf16[1024,2048]{1,0:T(8,128)(2,1)} async-done(((bf16[256,2048]{1,0:T(8,128)(2,1)}), bf16[1024,2048]{1,0:T(8,128)(2,1)}) %all-gather.6.cloned.1.call-update) | async-done | bytes 4194320 | tf_op jit(solution)/shard_map/all_gather | solution.py:59
  98.5 4.6 fusion.105
  103.1 3.9 copy.55
  107.0 4.0 copy.56
  111.1 27.0 %while.37 = (s32[]{:T(128)}, bf16[8,2,256,64]{2,3,1,0:T(8,128)(2,1)S(1)}, f32[8,2,256]{2,1,0:T(2,128)S(1)}, bf16[8,2,256,64]{2,3,1,0:T(8,128)(2,1)}, bf16[8,2,10...) while((s32[]{:T(128)}, ...), condition=%wide.region_6.7_spmd.clone, body=%wide.region_4.6_spmd.clone.sunk | while | flops 138411520 | bytes 8076385 | solution.py:81
  111.2 1.7 fusion.139
  114.6 1.7 fusion.139
  124.7 1.7 fusion.139
  139.8 5.1 all-gather.1
  149.9 35.3 %while.38 = (s32[]{:T(128)}, bf16[8,2,256,64]{2,3,1,0:T(8,128)(2,1)}, bf16[8,2,256,64]{2,3,1,0:T(8,128)(2,1)}, bf16[8,2,1024,64]{2,3,1,0:T(8,128)(2,1)}, f32[8,2...) while((s32[]{:T(128)}, ...), condition=%wide.region_10.11_spmd.clone, body=%wide.region_9.10_spmd.clone.sunk | while | flops 205520896 | bytes 7360625 | solution.py:134
  151.5 2.8 fusion.147
  155.9 2.8 fusion.147
  160.3 2.8 fusion.147
  164.7 2.8 fusion.147
  169.2 2.8 fusion.147
  173.6 2.8 fusion.147
  178.0 2.8 fusion.147
  182.4 2.8 fusion.147
  185.2 5.2 %all_gather.27 = bf16[8,2,1024]{2,1,0:T(2,128)(2,1)S(1)} all-gather(bf16[8,2,256]{2,1,0:T(2,128)(2,1)S(1)} %convert_element_type.107), channel_id=1, replica_groups=mesh['wide'=8,'narrow'=4] {'narrow'}, dimensions={2}, use_global_device_ids=true | all-gather | bytes 40960 | tf_op jit(solution)/shard_map/all_gather | solution.py:143
  190.4 5.3 %all_gather.25 = bf16[8,2,1024]{2,1,0:T(2,128)(2,1)S(1)} all-gather(bf16[8,2,256]{2,1,0:T(2,128)(2,1)S(1)} %convert_element_type.105), channel_id=1, replica_groups=mesh['wide'=8,'narrow'=4] {'narrow'}, dimensions={2}, use_global_device_ids=true | all-gather | bytes 40960 | tf_op jit(solution)/shard_map/all_gather | solution.py:140
  195.8 3.8 fusion.91
  199.6 3.9 copy.60
  204.5 44.2 %while.39 = (s32[]{:T(128)}, bf16[8,2,256,64]{2,3,1,0:T(8,128)(2,1)S(1)}, bf16[8,2,256,64]{2,3,1,0:T(8,128)(2,1)}, bf16[8,2,1024,64]{2,3,1,0:T(8,128)(2,1)}, bf1...) while((s32[]{:T(128)}, ...), condition=%wide.region_12.13_spmd.clone, body=%wide.region_11.12_spmd.clone.sunk | while | flops 273154048 | bytes 9888889 | solution.py:171
  204.7 1.7 multiply_divide_fusion.3
  206.4 1.7 fusion.155
  208.2 1.9 fusion.156
  210.3 1.7 multiply_divide_fusion.3
  211.9 1.7 fusion.155
  213.7 1.9 fusion.156
  215.8 1.7 multiply_divide_fusion.3
  217.5 1.7 fusion.155
  219.2 1.9 fusion.156
  221.3 1.7 multiply_divide_fusion.3
  223.0 1.7 fusion.155
  224.7 1.9 fusion.156
  226.8 1.7 multiply_divide_fusion.3
  228.5 1.7 fusion.155
  230.3 1.9 fusion.156
  232.3 1.7 multiply_divide_fusion.3
  234.0 1.7 fusion.155
  235.8 1.9 fusion.156
  237.9 1.7 multiply_divide_fusion.3
  239.6 1.7 fusion.155
  241.3 1.9 fusion.156
  243.4 1.7 multiply_divide_fusion.3
  245.1 1.7 fusion.155
  246.9 1.9 fusion.156
  248.8 7.5 %fusion.92 = f32[1024,3072]{0,1:T(8,128)} fusion(bf16[256,1024]{1,0:T(8,128)(2,1)S(1)} %copy-done.8, bf16[256,1024]{0,1:T(8,128)(2,1)} %bitcast.222, bf16[256,1024]{0,1:T(8,128)(2,1)S(1)} %bitcast.220, bf16[256,1024]{0,1:T(8,128)(2,1)} %bitcast.224), kind=kOutput, calls=%fused_computation.118 | convolution fusion | flops 1615331328 | bytes 14680064 | tf_op jit(solution)/shard_map/rd,re->de/dot_general | solution.py:178
  257.7 4.7 fusion.89
  264.1 5.6 %all-to-all-start.2 = ((bf16[8,32,1024]{2,1,0:T(8,128)(2,1)}), bf16[8,32,1024]{2,1,0:T(8,128)(2,1)S(1)}, u32[]{:S(2)}, u32[]{:S(2)}) async-start(bf16[8,32,1024]{2,1,0:T(8,128)(2,1)} %gather_fusion.4), calls=%async_computation.2 | async-start | bytes 1048576 | tf_op jit(solution)/shard_map/all_to_all | solution.py:188
  269.8 17.0 %all-to-all-done.2 = bf16[8,32,1024]{2,1,0:T(8,128)(2,1)S(1)} async-done(((bf16[8,32,1024]{2,1,0:T(8,128)(2,1)}), bf16[8,32,1024]{2,1,0:T(8,128)(2,1)S(1)}, u32[]{:S(2)}, u32[]{:S(2)}) %all-to-all-start.2) | async-done | bytes 524320 | tf_op jit(solution)/shard_map/all_to_all | solution.py:188
  288.1 55.2 %reduce-scatter.5.cloned.1.call-done = f32[1024,32]{0,1:T(8,128)} async-done(((f32[1024,1024]{0,1:T(8,128)}), f32[1024,32]{0,1:T(8,128)}) %reduce-scatter.5.cloned.1.call-update) | async-done | bytes 131088 | tf_op jit(solution)/shard_map/reduce_scatter | solution.py:192
  343.4 157.4 %reduce-scatter.3.cloned.1.call-done = f32[1024,96]{0,1:T(8,128)} async-done(((f32[1024,3072]{0,1:T(8,128)}), f32[1024,96]{0,1:T(8,128)}) %reduce-scatter.3.cloned.1.call-update) | async-done | bytes 393232 | tf_op jit(solution)/shard_map/reduce_scatter | solution.py:191
  (169 shorter events, 57.0 us)
Async XLA Ops:
  7.2 131.0 %copy-start = (bf16[1024,1024]{1,0:T(8,128)(2,1)S(1)}, bf16[1024,1024]{1,0:T(8,128)(2,1)}, u32[]{:S(2)}) copy-start(bf16[1024,1024]{1,0:T(8,128)(2,1)} %param.22) | copy-start | bytes 6291460
  7.2 10.7 %copy-start.16 = (s32[1,8]{1,0:T(1,128)S(1)}, s32[1,8]{1,0:T(1,128)}, u32[]{:S(2)}) copy-start(s32[1,8]{1,0:T(1,128)} %param.18) | copy-start | bytes 100
  7.2 26.0 %copy-start.13 = (f32[1024]{0:T(1024)S(1)}, f32[1024]{0:T(1024)}, u32[]{:S(2)}) copy-start(f32[1024]{0:T(1024)} %param.20) | copy-start | bytes 12292
  10.6 21.8 %all-to-all-start.1 = ((bf16[8,32,1024]{2,1,0:T(8,128)(2,1)}), bf16[8,32,1024]{2,1,0:T(8,128)(2,1)S(1)}, u32[]{:S(2)}, u32[]{:S(2)}) async-start(bf16[8,32,1024]{2,1,0:T(8,128)(2,1)} %gather_fusion.2), calls=%async_computation.1 | async-start | bytes 1048576 | tf_op jit(solution)/shard_map/all_to_all | solution.py:42
  17.8 48.3 %all-gather.8.cloned.1.call-start = ((), (), s32[]{:S(2)}) async-start(), calls=%async_computation.6 | async-start | bytes 2621440 | tf_op jit(solution)/shard_map/all_gather | solution.py:136
  32.9 105.2 %copy-start.2 = (bf16[8,32,1024]{2,1,0:T(8,128)(2,1)}, bf16[8,32,1024]{2,1,0:T(8,128)(2,1)S(1)}, u32[]{:S(2)}) copy-start(bf16[8,32,1024]{2,1,0:T(8,128)(2,1)S(1)} %gather_fusion.3) | copy-start | bytes 1572868
  33.4 4.8 copy-start.7
  38.2 1.2 copy-start.6
  40.6 2.6 copy-start.15
  40.6 7.5 %copy-start.14 = (s32[8,3]{0,1:T(4,128)S(1)}, s32[8,3]{0,1:T(4,128)}, u32[]{:S(2)}) copy-start(s32[8,3]{0,1:T(4,128)} %param.19) | copy-start | bytes 292
  40.6 20.4 %copy-start.5 = (bf16[256,1024]{1,0:T(8,128)(2,1)S(1)}, bf16[256,1024]{1,0:T(8,128)(2,1)}, u32[]{:S(2)}) copy-start(bf16[256,1024]{1,0:T(8,128)(2,1)} %get-tuple-element.313) | copy-start | bytes 1572868
  40.6 57.9 %all-gather.6.cloned.1.call-start = ((), (), s32[]{:S(2)}) async-start(), calls=%async_computation.5 | async-start | bytes 5242880 | tf_op jit(solution)/shard_map/all_gather | solution.py:59
  44.4 10.0 %all-to-all-start = ((bf16[8,1,32]{2,1,0:T(2,128)(2,1)}), bf16[8,1,32]{2,1,0:T(2,128)(2,1)S(1)}, u32[]{:S(2)}, u32[]{:S(2)}) async-start(bf16[8,1,32]{2,1,0:T(2,128)(2,1)} %copy.53), calls=%async_computation | async-start | bytes 8192 | tf_op jit(solution)/shard_map/all_to_all | solution.py:43
  48.0 151.6 %all-gather.10.cloned.1.call-start = ((), (), s32[]{:S(2)}) async-start(), calls=%async_computation.7 | async-start | bytes 2621440 | tf_op jit(solution)/shard_map/all_gather | solution.py:137
  138.1 9.7 %copy-start.4 = (bf16[8,2,256,64]{2,3,1,0:T(8,128)(2,1)}, bf16[8,2,256,64]{2,3,1,0:T(8,128)(2,1)S(1)}, u32[]{:S(2)}) copy-start(bf16[8,2,256,64]{2,3,1,0:T(8,128)(2,1)S(1)} %get-tuple-element.141) | copy-start | bytes 1572868
  138.1 0.7 copy-start.12
  146.7 1.0 copy-start.11
  147.7 195.6 %reduce-scatter.5.cloned.1.call-start = ((), (), s32[]{:S(2)}) async-start(), calls=%async_computation.9 | async-start | bytes 4325376 | tf_op jit(solution)/shard_map/reduce_scatter | solution.py:192
  199.6 301.2 %reduce-scatter.3.cloned.1.call-start = ((), (), s32[]{:S(2)}) async-start(), calls=%async_computation.8 | async-start | bytes 12976128 | tf_op jit(solution)/shard_map/reduce_scatter | solution.py:191
  204.5 44.2 %copy-start.8 = (bf16[256,1024]{1,0:T(8,128)(2,1)S(1)}, bf16[256,1024]{1,0:T(8,128)(2,1)}, u32[]{:S(2)}) copy-start(bf16[256,1024]{1,0:T(8,128)(2,1)} %copy-done.7) | copy-start | bytes 1572868
  256.3 1.0 copy-start.3
  256.3 1.2 copy-start.9
  256.3 1.4 copy-start.10
  262.4 7.3 %copy-start.17 = (s32[1,8]{1,0:T(1,128)S(1)}, s32[1,8]{1,0:T(1,128)}, u32[]{:S(2)}) copy-start(s32[1,8]{1,0:T(1,128)} %param.17) | copy-start | bytes 100
  262.4 238.3 %copy-start.1 = (bf16[1024,1024]{1,0:T(8,128)(2,1)S(1)}, bf16[1024,1024]{1,0:T(8,128)(2,1)}, u32[]{:S(2)}) copy-start(bf16[1024,1024]{1,0:T(8,128)(2,1)} %param.22) | copy-start | bytes 6291460
  264.1 22.6 %all-to-all-start.2 = ((bf16[8,32,1024]{2,1,0:T(8,128)(2,1)}), bf16[8,32,1024]{2,1,0:T(8,128)(2,1)S(1)}, u32[]{:S(2)}, u32[]{:S(2)}) async-start(bf16[8,32,1024]{2,1,0:T(8,128)(2,1)} %gather_fusion.4), calls=%async_computation.2 | async-start | bytes 1048576 | tf_op jit(solution)/shard_map/all_to_all | solution.py:188
Sparse Core Ops, SparseCore 0:
  40.7 21.6 all-gather.7
  64.0 34.4 all-gather.5
  147.9 22.5 all-gather.9
  199.7 143.6 reduce-scatter.4
  349.8 150.8 reduce-scatter.2
where the time goes:
time: 510 us; the launch traced here: 507 us
  waiting for transfers between devices  278 us (55%)
  matrix products  126 us (25%)
  local copies, waits for them, and re-layouts  42.7 us (8%)
  blocking collectives  20.8 us (4%)
  starting transfers between devices  16.7 us (3%)
  between operations  14.1 us (3%)
  other arithmetic  8.14 us (2%)
    reduce_scatter x1, waiting for transfers between devices, body(): lax.psum_scatter(qkv_part, ('wide', 'narrow'), scatter_dimension=1, tiled...  157 us
    reduce_scatter x1, waiting for transfers between devices, body(): lax.psum_scatter(out_part, ('wide', 'narrow'), scatter_dimension=1, tiled...  55.2 us
    dot_general x24, matrix products, attend_probs(): jnp.einsum('hqd,hkd->hqk', query_part, key_part, preferred_element_type=j...  38.5 us
    all_gather x1, waiting for transfers between devices, body(): lax.all_gather(projected[:, width:], 'narrow', axis=0, tiled=True)  28.4 us
    dot_general x8, matrix products, backward_block(): jnp.einsum('hqk,hkd->hqd', logit_grad, key_part, preferred_element_type=j...  22.3 us
    all_to_all x1, waiting for transfers between devices, body(): lax.all_to_all(returning, 'wide', split_axis=0, concat_axis=0, tiled=True)  17 us
    dot_general x8, matrix products, reverse_block(): jnp.einsum('hqk,hqd->hkd', probs_back.astype(jnp.bfloat16), upstream_part...  15.1 us
    all_to_all x1, waiting for transfers between devices, body(): lax.all_to_all(outgoing, 'wide', split_axis=0, concat_axis=0, tiled=True)  14.4 us
  transfers between devices with their start and end apart: 8, of which 6 were waited for; matrix products, arithmetic and copies ran while one was open for 24% of the time, Pallas kernels for 0%

commit v1 on v0

v1 whole, which is shorter than its diff:
```python
import jax
import jax.numpy as jnp
from jax import lax
from jax.experimental import pallas as pl
from jax.experimental.pallas import tpu as pltpu
from jax.sharding import PartitionSpec as P

HEADS = 16
LANES = 128
epsilon = 1e-06
loss_scale = 64.0
log2e = 1.4426950408889634
far = 2.0**100
bf16 = jnp.bfloat16
f32 = jnp.float32


def vmem():
    return pl.BlockSpec(memory_space=pltpu.VMEM)


def smem():
    return pl.BlockSpec(memory_space=pltpu.SMEM)


def call(kernel, shapes, specs, **more):
    params = pltpu.CompilerParams(vmem_limit_bytes=56 * 2**20)
    return pl.pallas_call(kernel, out_shape=shapes, in_specs=specs, compiler_params=params, **more)


def split(values):
    high = values.astype(bf16)
    return high, (values - high.astype(f32)).astype(bf16)


def pack_kernel(dest, rows, grades, out):
    count, piece, width = rows.shape
    for b in range(count):
        out[dest[0, b], :, :width] = rows[b]
        out[dest[0, b], :, width:] = jnp.broadcast_to(grades[b], (piece, LANES)).astype(bf16)


def norm_kernel(source, incoming, gain, score, out, inverse_out, rows_out):
    count, piece, wide = incoming.shape
    width = wide - LANES
    lane = lax.broadcasted_iota(jnp.int32, (piece, LANES), 1)
    for c in range(count):
        block = incoming[source[0, c]]
        rows = block[:, :width]
        values = rows.astype(f32)
        inverse = lax.rsqrt(jnp.mean(values * values, axis=1, keepdims=True) + epsilon)
        out[c, :, :width] = (values * inverse * gain[...]).astype(bf16)
        base = jnp.sum(values * score[...], axis=1, keepdims=True)
        high = base.astype(bf16).astype(f32)
        middle = (base - high).astype(bf16).astype(f32)
        low = base - high - middle
        info = jnp.where(lane == 1, high, block[:, width:].astype(f32))
        info = jnp.where(lane == 2, middle, info)
        info = jnp.where(lane == 3, low, info)
        out[c, :, width:] = info.astype(bf16)
        inverse_out[c] = inverse
        rows_out[c] = rows


def project_kernel(x, weights, qk_out, z_out):
    both = qk_out.shape[1]
    out = jnp.dot(x[:, : x.shape[1] - LANES], weights[...], preferred_element_type=f32)
    qk_out[...] = out[:, :both].astype(bf16)
    z_out[...] = out[:, both:]


def forward_kernel(query, key, z, seg_col, seg_all, a_out, e_out, stat_out, zrow_out, kx, zt):
    total = key.shape[0]
    rows = query.shape[0]
    heads = e_out.shape[0]
    half = LANES // 2

    @pl.when(pl.program_id(0) == 0)
    def _():
        lane = lax.broadcasted_iota(jnp.int32, (total, LANES), 1)
        away = jnp.where(lane == seg_all[...], 0.0, -far).astype(bf16)
        for p in range(heads // 2):
            kx[p, :, :LANES] = key[:, p * LANES : (p + 1) * LANES]
            kx[p, :, LANES:] = away
        turned = z[...].T
        zt[...] = turned[:8] + turned[8:16]
        zrow_out[...] = zt[...]

    lane = lax.broadcasted_iota(jnp.int32, (rows, LANES), 1)
    mine = (lane == seg_col[...]).astype(f32).astype(bf16)
    stats = jnp.zeros((rows, LANES), f32)
    zsum = jnp.zeros((rows, 1), f32)
    for p in range(heads // 2):
        parts = []
        for s in range(2):
            h = 2 * p + s
            own = query[:, p * LANES : (p + 1) * LANES]
            own = jnp.where((lane >= half) == (s == 1), own, jnp.zeros_like(own))
            logits = lax.dot_general(
                jnp.concatenate([own, mine], axis=1),
                kx[p],
                (((1,), (1,)), ((), ())),
                preferred_element_type=f32,
            )
            weights = jnp.exp2(logits * log2e)
            e_out[h] = weights.astype(bf16)
            zrow = zt[h : h + 1, :]
            inverse = 1.0 / jnp.sum(weights, axis=1, keepdims=True)
            zeta = jnp.sum(weights * zrow, axis=1, keepdims=True) * inverse
            centred = (weights * (zrow - zeta)).astype(bf16)
            part = jnp.dot(centred, kx[p, :, :LANES], preferred_element_type=f32) * inverse
            parts.append(part)
            stats = jnp.where(lane == h, zeta, stats)
            stats = jnp.where(lane == heads + h, inverse, stats)
            zsum = zsum + zeta
        a_out[:, p * LANES : (p + 1) * LANES] = jnp.where(lane >= half, parts[1], parts[0])
    stat_out[...] = jnp.where(lane == 2 * heads, zsum, stats)


def backward_kernel(
    e, stat, query, a, zrow, s_col, s_row, g_col, g_row, t_col, t_row,
    key_out, c_out, qg_out, sg_out, key_acc, c_acc,
):
    heads, rows, total = e.shape
    half = LANES // 2
    scale = half**-0.5
    step = pl.program_id(0)

    @pl.when(step == 0)
    def _():
        key_acc[...] = jnp.zeros_like(key_acc)
        c_acc[...] = jnp.zeros_like(c_acc)

    lane = lax.broadcasted_iota(jnp.int32, (rows, LANES), 1)
    same = t_col[...] == t_row[...]
    gains = g_row[...]
    spread = gains - g_col[...]
    margin = s_col[...] - s_row[...]
    margin = jnp.where(spread > 0.0, margin, -margin)
    pulls = spread / (1.0 + jnp.exp(-margin))
    pulls = jnp.sum(jnp.where(same, pulls, 0.0), axis=1, keepdims=True)
    norm = jnp.sum(jnp.where(same, gains, 0.0), axis=1, keepdims=True)
    grad = loss_scale * pulls / norm
    sg_out[...] = grad
    qg_out[...] = (a[...] * (grad * scale)).astype(bf16)
    stats = stat[...]
    for h in range(heads):
        p, s = h // 2, h % 2
        zeta = stats[:, h : h + 1]
        scaled = e[h].astype(f32) * (stats[:, heads + h : heads + h + 1] * grad)
        c_acc[h : h + 1, :] += jnp.sum(scaled, axis=0, keepdims=True)
        centred = (scaled * (zrow[h : h + 1, :] - zeta)).astype(bf16)
        own = query[:, p * LANES : (p + 1) * LANES]
        own = jnp.where((lane >= half) == (s == 1), own, jnp.zeros_like(own))
        key_acc[p * LANES : (p + 1) * LANES, :] += lax.dot_general(
            own, centred, (((0,), (0,)), ((), ())), preferred_element_type=f32
        )

    @pl.when(step == pl.num_programs(0) - 1)
    def _():
        key_out[...] = key_acc[...].astype(bf16)
        c_out[...] = c_acc[...]


def tail_kernel(source, normed_grad, rows, inverse, grad, gain, score, out):
    count, piece, width = out.shape
    for c in range(count):
        part = pl.ds(c * piece, piece)
        scaled = normed_grad[part, :] * gain[...]
        values = rows[c].astype(f32)
        inv = inverse[c]
        mean = jnp.mean(scaled * values, axis=1, keepdims=True)
        total = grad[part, :] * score[...] + inv * scaled - values * (inv * inv * inv * mean)
        out[source[0, c]] = total.astype(bf16)


def body(rows, grades, block_dest, block_source, lengths, gain, w_qkv, w_out, w_score):
    wide = lax.axis_size("wide")
    narrow = lax.axis_size("narrow")
    wide_index = lax.axis_index("wide")
    narrow_index = lax.axis_index("narrow")
    local, width = rows.shape
    piece = local // wide
    head_size = width // HEADS
    heads = HEADS // narrow
    own = heads * head_size
    total = local * narrow
    chunk = width // wide
    scale = head_size**-0.5
    order = jnp.bitwise_xor(narrow_index, jnp.arange(narrow, dtype=jnp.int32))

    def swap(values, m):
        return lax.ppermute(values, "narrow", [(i, i ^ m) for i in range(narrow)])

    def spread(values):
        held = [values]
        step = 1
        while step < narrow:
            held = held + [None] * len(held)
            held[step] = swap(values, step)
            step *= 2
        for m in range(narrow):
            if held[m] is None:
                top = 1 << (m.bit_length() - 1)
                held[m] = swap(held[top], m ^ top)
        return held

    u = jnp.sum(w_out.astype(f32) * w_score[None, :], axis=1)
    w_q = w_qkv[:, :width].reshape(width, narrow, own)[:, order].reshape(width, width)
    w_k = w_qkv[:, width : 2 * width].reshape(width, narrow, own)[:, order].reshape(width, width)
    head_of = jnp.arange(width, dtype=jnp.int32) // head_size
    head_order = (order[:, None] * heads + jnp.arange(heads, dtype=jnp.int32)[None, :]).reshape(-1)
    u_heads = jnp.where(head_of[:, None] == head_order[None, :], u[:, None], 0.0)
    u_high, u_low = split(u_heads)
    g_both = jnp.dot(
        w_qkv[:, 2 * width :], jnp.concatenate([u_high, u_low], axis=1), preferred_element_type=f32
    )
    g_all = g_both[:, :HEADS] + g_both[:, HEADS:]
    g_high, g_low = split(g_all[:, :heads])
    pad = jnp.zeros((width, 8 - heads), bf16)
    g_own = jnp.concatenate([g_high, pad, g_low, pad, jnp.zeros((width, LANES - 16), bf16)], axis=1)
    weights = jnp.concatenate([w_q[:, :own] * bf16(scale), w_k[:, :own], g_own], axis=1)

    outgoing = call(
        pack_kernel,
        jax.ShapeDtypeStruct((wide, piece, width + LANES), bf16),
        [smem(), vmem(), vmem()],
    )(
        block_dest,
        rows.reshape(wide, piece, width),
        grades.astype(f32).reshape(wide, piece, 1),
    )
    incoming = lax.all_to_all(outgoing, "wide", split_axis=0, concat_axis=0, tiled=True)
    normx, inverse, work = call(
        norm_kernel,
        (
            jax.ShapeDtypeStruct((wide, piece, width + LANES), bf16),
            jax.ShapeDtypeStruct((wide, piece, 1), f32),
            jax.ShapeDtypeStruct((wide, piece, width), bf16),
        ),
        [smem(), vmem(), vmem(), vmem()],
    )(block_source, incoming, gain[None, :], w_score[None, :])
    x_all = jnp.concatenate(spread(normx.reshape(local, width + LANES)), axis=0)
    qk, z = call(
        project_kernel,
        (
            jax.ShapeDtypeStruct((total, 2 * own), bf16),
            jax.ShapeDtypeStruct((total, LANES), f32),
        ),
        [
            pl.BlockSpec((local, width + LANES), lambda i: (i, 0)),
            pl.BlockSpec((width, 2 * own + LANES), lambda i: (0, 0)),
        ],
        grid=(narrow,),
        out_specs=(
            pl.BlockSpec((local, 2 * own), lambda i: (i, 0)),
            pl.BlockSpec((local, LANES), lambda i: (i, 0)),
        ),
    )(x_all, weights)

    bounds = jnp.cumsum(lax.dynamic_index_in_dim(lengths, wide_index, 0, keepdims=False))
    positions = (order[:, None] * local + jnp.arange(local, dtype=jnp.int32)[None, :]).reshape(-1)
    segment = jnp.sum((positions[:, None] >= bounds[None, :]).astype(jnp.int32), axis=1)

    column = pl.BlockSpec((local, 1), lambda i: (i, 0))
    line = pl.BlockSpec((1, total), lambda i: (0, 0))
    a, e, stat, zrow = call(
        forward_kernel,
        (
            jax.ShapeDtypeStruct((total, own), f32),
            jax.ShapeDtypeStruct((heads, total, total), bf16),
            jax.ShapeDtypeStruct((total, LANES), f32),
            jax.ShapeDtypeStruct((8, total), f32),
        ),
        [
            pl.BlockSpec((local, own), lambda i: (i, 0)),
            pl.BlockSpec((total, own), lambda i: (0, 1)),
            pl.BlockSpec((total, LANES), lambda i: (0, 0)),
            column,
            pl.BlockSpec((total, 1), lambda i: (0, 0)),
        ],
        grid=(narrow,),
        out_specs=(
            pl.BlockSpec((local, own), lambda i: (i, 0)),
            pl.BlockSpec((heads, local, total), lambda i: (0, i, 0)),
            pl.BlockSpec((local, LANES), lambda i: (i, 0)),
            pl.BlockSpec((8, total), lambda i: (0, 0)),
        ),
        scratch_shapes=[
            pltpu.VMEM((heads // 2, total, 2 * LANES), bf16),
            pltpu.VMEM((8, total), f32),
        ],
    )(qk, qk, z, segment[:, None], segment[:, None])

    info = x_all[:, width : width + 4].astype(f32)
    partial = stat[:, 2 * heads].reshape(narrow, local)
    step = 1
    while step < narrow:
        other = swap(partial, step)
        partial = partial + jnp.stack([other[m ^ step] for m in range(narrow)])
        step *= 2
    scores = info[:, 1] + info[:, 2] + info[:, 3] + partial.reshape(total)
    gains = jnp.exp2(info[:, 0])

    a_bf = a.astype(bf16)
    a_rows = [a_bf[:local]] + [swap(a_bf[m * local : (m + 1) * local], m) for m in range(1, narrow)]
    a_rows = jnp.concatenate(a_rows, axis=1)

    key_t, c_t, query_grad, score_grad = call(
        backward_kernel,
        (
            jax.ShapeDtypeStruct((own, total), bf16),
            jax.ShapeDtypeStruct((8, total), f32),
            jax.ShapeDtypeStruct((total, own), bf16),
            jax.ShapeDtypeStruct((total, 1), f32),
        ),
        [
            pl.BlockSpec((heads, local, total), lambda i: (0, i, 0)),
            pl.BlockSpec((local, LANES), lambda i: (i, 0)),
            pl.BlockSpec((local, own), lambda i: (i, 0)),
            pl.BlockSpec((local, own), lambda i: (i, 0)),
            pl.BlockSpec((8, total), lambda i: (0, 0)),
            column,
            line,
            column,
            line,
            column,
            line,
        ],
        grid=(narrow,),
        out_specs=(
            pl.BlockSpec((own, total), lambda i: (0, 0)),
            pl.BlockSpec((8, total), lambda i: (0, 0)),
            pl.BlockSpec((local, own), lambda i: (i, 0)),
            column,
        ),
        scratch_shapes=[pltpu.VMEM((own, total), f32), pltpu.VMEM((8, total), f32)],
    )(
        e, stat, qk, a, zrow,
        scores[:, None], scores[None, :],
        gains[:, None], gains[None, :],
        segment[:, None], segment[None, :],
    )

    c_high, c_low = split(c_t[:heads])
    keys_c = jnp.concatenate([key_t, c_high, c_low, jnp.zeros((8, total), bf16)], axis=0)
    k_rows = [keys_c[:, :local]]
    k_rows += [swap(keys_c[:, m * local : (m + 1) * local], m) for m in range(1, narrow)]
    c_rows = jnp.concatenate(
        [r[own : own + heads].astype(f32) + r[own + heads : own + 2 * heads].astype(f32) for r in k_rows]
    )
    k_rows = jnp.concatenate([r[:own] for r in k_rows], axis=0)

    normed_all = x_all[:, :width]
    grad_q = lax.dot_general(
        query_grad, normed_all, (((0,), (0,)), ((), ())), preferred_element_type=f32
    )
    grad_k = jnp.dot(keys_c, normed_all, preferred_element_type=f32)
    m_own = grad_k[own : own + heads] + grad_k[own + heads : own + 2 * heads]
    w_v = lax.dynamic_slice_in_dim(w_qkv, 2 * width + narrow_index * own, own, axis=1)
    m_high, m_low = split(m_own)
    v_both = jnp.dot(jnp.concatenate([m_high, m_low]), w_v, preferred_element_type=f32)
    v_heads = v_both[:heads] + v_both[heads:]
    own_head = jnp.arange(own, dtype=jnp.int32) // head_size
    v_own = jnp.sum(
        jnp.where(own_head[None, :] == jnp.arange(heads, dtype=jnp.int32)[:, None], v_heads, 0.0), axis=0
    )

    def to_chunks(values):
        return values.reshape(-1, wide, chunk).transpose(1, 0, 2)

    v_high, v_low = split(v_own)
    v_lines = jnp.concatenate([v_high, v_low]).reshape(1, -1, chunk)
    count_v = v_lines.shape[1]
    blocks = [
        to_chunks(jnp.concatenate([grad_q, grad_k[:own]]).astype(bf16)),
        to_chunks(jnp.concatenate([m_high, m_low])),
        jnp.broadcast_to(v_lines, (wide, count_v, chunk)),
    ]
    fill = -(2 * own + 2 * heads + count_v) % 16
    blocks.append(jnp.zeros((wide, fill, chunk), bf16))
    terms = lax.all_to_all(
        jnp.concatenate(blocks, axis=1), "wide", split_axis=0, concat_axis=0, tiled=True
    )
    summed = jnp.sum(terms.astype(f32), axis=0)

    def both(values):
        n = values.shape[0] // 2
        return values[:n] + values[n:]

    at = 2 * own + 2 * heads
    m_high, m_low = split(both(summed[2 * own : at]))
    v_sum = both(summed[at : at + count_v])
    v_high, v_low = split(v_sum)
    send = jnp.concatenate([summed[: 2 * own].astype(bf16), m_high, m_low, v_high, v_low], axis=0)
    gathered = jnp.stack(spread(send))[order]
    q_cols = gathered[:, :own].reshape(width, chunk)
    k_cols = gathered[:, own : 2 * own].reshape(width, chunk)
    m_all = gathered[:, 2 * own : 2 * own + heads].astype(f32) + gathered[:, 2 * own + heads : at].astype(f32)
    m_rows = jnp.broadcast_to(m_all.reshape(HEADS, 1, chunk), (HEADS, head_size, chunk))
    v_cols = (m_rows.reshape(width, chunk) * u[:, None]).astype(bf16)
    half_v = count_v // 2
    v_all = gathered[:, at : at + half_v].astype(f32) + gathered[:, at + half_v : at + count_v].astype(f32)
    v_all = v_all.reshape(width)
    columns = 3 * width // (wide * narrow)
    full = jnp.concatenate([q_cols, k_cols, v_cols], axis=0).reshape(wide, narrow, columns, chunk)
    mine = lax.dynamic_index_in_dim(full, narrow_index, 1, keepdims=False)
    parts = lax.all_to_all(mine, "wide", split_axis=0, concat_axis=0, tiled=True)
    grad_qkv = parts.astype(f32).transpose(0, 2, 1).reshape(width, columns)
    out_columns = width // (wide * narrow)
    place = (wide_index * narrow + narrow_index) * out_columns
    grad_out = v_all[:, None] * lax.dynamic_slice_in_dim(w_score, place, out_columns)[None, :]

    own_grad = score_grad[:local]
    normed_grad = own_grad * scale * jnp.einsum("rd,ed->re", a_rows, w_q, preferred_element_type=f32)
    normed_grad = normed_grad + jnp.einsum("dr,ed->re", k_rows, w_k, preferred_element_type=f32)
    normed_grad = normed_grad + jnp.einsum(
        "hr,eh->re", c_rows, g_all, precision=lax.Precision.HIGHEST, preferred_element_type=f32
    )
    returning = call(
        tail_kernel,
        jax.ShapeDtypeStruct((wide, piece, width), bf16),
        [smem()] + [vmem()] * 6,
    )(block_source, normed_grad, work, inverse, own_grad, gain[None, :], w_score[None, :])
    arrived = lax.all_to_all(returning, "wide", split_axis=0, concat_axis=0, tiled=True)
    grad_rows = arrived[block_dest[0]].reshape(local, width)
    return (grad_rows, grad_qkv, grad_out)


def solution(mesh):
    both = ("wide", "narrow")
    placed = (P(both, None), P(both), P(both, None), P(both, None), P(), P(), P(), P(), P())
    return jax.shard_map(
        body,
        mesh=mesh,
        in_specs=placed,
        out_specs=(P(both, None), P(None, both), P(None, both)),
        check_vma=False,
    )
```

time: 510 us -> 183 us (0.36)
  waiting for transfers between devices: 278 us -> 43.2 us
  matrix products: 126 us -> 12.4 us
  Pallas kernels: 0 us -> 35.6 us
  blocking collectives: 20.8 us -> 0 us
  other arithmetic: 8.14 us -> 21.2 us
  between operations: 14.1 us -> 1.24 us
  starting transfers between devices: 16.7 us -> 25.7 us
    reduce_scatter x2 -> x0, waiting for transfers between devices: 213 us -> none  [the longest x1 157 us: body(): lax.psum_scatter(qkv_part, ('wide', 'narrow'), scatter_dimension=1, tiled...]
    dot_general x64 -> x7, matrix products: 126 us -> 12.4 us  [the longest x1 2.75 us: body(): jnp.einsum('rd,ed->re', a_rows, w_q, preferred_element_type=f32)]
    pallas_call x0 -> x6, Pallas kernels: none -> 35.6 us  [the longest x1 12.3 us: body(): call(forward_kernel, (jax.ShapeDtypeStruct((total, own), f32), jax.ShapeD...]
    all_gather x3 -> x0, waiting for transfers between devices: 28.4 us -> none  [the longest x1 28.4 us: body(): lax.all_gather(projected[:, width:], 'narrow', axis=0, tiled=True)]
    all_gather x4 -> x0, blocking collectives: 20.8 us -> none  [the longest x1 5.33 us: body(): lax.all_gather(totals_blocks.astype(jnp.bfloat16), 'narrow', axis=2, tile...]
    slice x8 -> x13, local copies, waits for them, and re-layouts: 21.3 us -> 7.69 us  [the longest x1 4.66 us: body(): w_qkv[:, width:2 * width].reshape(width, narrow, own)[:, order]]
    all_to_all x1 -> x2, waiting for transfers between devices: 5.81 us -> 16.5 us  [the longest x1 9.06 us: body(): lax.all_to_all(jnp.concatenate(blocks, axis=1), 'wide', split_axis=0, con...]
    all_to_all x1, waiting for transfers between devices: 17 us -> 8.31 us  [body(): lax.all_to_all(returning, 'wide', split_axis=0, concat_axis=0, tiled=True)]
  transfers between devices with their start and end apart: 8 -> 18, of which waited for: 6 -> 7; matrix products, arithmetic and copies ran while one was open for 24% -> 35% of each run, Pallas kernels for 0% -> 8%
where the time goes in v1:
time: 183 us; the launch traced here: 182 us
  waiting for transfers between devices  43.2 us (24%)
  local copies, waits for them, and re-layouts  42.3 us (23%)
  Pallas kernels  35.6 us (19%)
  starting transfers between devices  25.7 us (14%)
  other arithmetic  21.2 us (12%)
  matrix products  12.4 us (7%)
    pallas_call x1, Pallas kernels, body(): call(forward_kernel, (jax.ShapeDtypeStruct((total, own), f32), jax.ShapeD...  12.3 us
    pallas_call x1, Pallas kernels, body(): call(backward_kernel, (jax.ShapeDtypeStruct((own, total), bf16), jax.Shap...  11.1 us
    unnamed x49, local copies, waits for them, and re-layouts  10.1 us
    all_to_all x1, waiting for transfers between devices, body(): lax.all_to_all(outgoing, 'wide', split_axis=0, concat_axis=0, tiled=True)  9.83 us
    all_to_all x1, waiting for transfers between devices, body(): lax.all_to_all(jnp.concatenate(blocks, axis=1), 'wide', split_axis=0, con...  9.06 us
    ppermute x14, waiting for transfers between devices, swap(): return lax.ppermute(values, 'narrow', [(i, i ^ m) for i in range(narrow)])  8.6 us
    all_to_all x1, waiting for transfers between devices, body(): lax.all_to_all(returning, 'wide', split_axis=0, concat_axis=0, tiled=True)  8.31 us
    ppermute x14, starting transfers between devices, swap(): return lax.ppermute(values, 'narrow', [(i, i ^ m) for i in range(narrow)])  7.43 us
  transfers between devices with their start and end apart: 18, of which 7 were waited for; matrix products, arithmetic and copies ran while one was open for 35% of the time, Pallas kernels for 8%

profile of v1, /device:TPU:0, one launch (start us, length us, event | category | flops | bytes accessed | tf_op | source)
XLA Modules:
  0.0 181.7 jit_solution(5712658796450082025)
XLA Ops:
  0.7 0.8 convert_element_type.128
  1.5 0.9 reshape.331.grades
  2.4 2.0 %shard_map.112 = bf16[8,32,1152]{2,1,0:T(8,128)(2,1)} custom-call(s32[1,8]{1,0:T(1,128)} %dest.1, bf16[8,32,1024]{2,1,0:T(8,128)(2,1)} %bitcast.113, f32[8,32,1]{2,1,0:T(8,128)} %reshape.331.grades), custom_call_target="tpu_custom_call" | custom-call | tf_op jit(solution)/shard_map/pallas_call | solution.py:224
  4.4 7.3 %all-to-all-start = ((bf16[8,32,1152]{2,1,0:T(8,128)(2,1)}), bf16[8,32,1152]{2,1,0:T(8,128)(2,1)S(1)}, u32[]{:S(2)}, u32[]{:S(2)}) async-start(bf16[8,32,1152]{2,1,0:T(8,128)(2,1)} %shard_map.112), calls=%async_computation | async-start | bytes 1179648 | tf_op jit(solution)/shard_map/all_to_all | solution.py:233
  13.1 4.7 %fusion.76 = (bf16[1024,1024]{1,0:T(8,128)(2,1)}, bf16[1024,1024]{1,0:T(8,128)(2,1)}) fusion(bf16[1024,3072]{1,0:T(8,128)(2,1)} %param.15), kind=kLoop, calls=%fused_computation.144 | loop fusion | bytes 8388608 | tf_op jit(solution)/shard_map/slice | solution.py:210
  17.7 9.8 %all-to-all-done.incoming = bf16[8,32,1152]{2,1,0:T(8,128)(2,1)S(1)} async-done(((bf16[8,32,1152]{2,1,0:T(8,128)(2,1)}), bf16[8,32,1152]{2,1,0:T(8,128)(2,1)S(1)}, u32[]{:S(2)}, u32[]{:S(2)}) %all-to-all-start) | async-done | bytes 589856 | tf_op jit(solution)/shard_map/all_to_all | solution.py:233
  27.5 0.8 copy-done.6
  28.4 2.4 %shard_map.113 = (bf16[8,32,1152]{2,1,0:T(8,128)(2,1)}, f32[8,32,1]{2,1,0:T(8,128)}, bf16[8,32,1024]{2,1,0:T(8,128)(2,1)}) custom-call(s32[1,8]{1,0:T(1,128)} %source.3, bf16[8,32,1152]{2,1,0:T(8,128)(2,1)} %copy-done.6, f32[1,1024]{1,0:T(1,128)} %bitcast.129, f32[1,1024]{1,0:T(1,128)} %bitcast.120), custom_call_target="tpu_custom_call" | custom-call | tf_op jit(solution)/shard_map/pallas_call | solution.py:234
  30.8 1.5 collective-permute-start.1
  32.4 2.9 %copy.103 = bf16[1024,1024]{0,1:T(8,128)(2,1)S(1)} copy(bf16[1024,1024]{1,0:T(8,128)(2,1)} %get-tuple-element.41) | data formatting | bytes 4194304
  35.2 2.6 %copy.90 = bf16[1024,4,256]{2,0,1:T(8,128)(2,1)} copy(bf16[1024,4,256]{0,2,1:T(8,128)(2,1)S(1)} %bitcast.102) | data formatting | bytes 4194304 | tf_op jit(solution)/shard_map/reshape | solution.py:210
  37.8 2.3 %gather_fusion.1 = bf16[4,1024,256]{2,1,0:T(8,128)(2,1)S(1)} fusion(bf16[1024,4,256]{2,0,1:T(8,128)(2,1)} %copy.90, s32[1024]{0:T(1024)S(1)} %pad_clamp_fusion.1), kind=kCustom, calls=%fused_computation.1 | custom fusion | bytes 4194320 | tf_op jit(solution)/shard_map/gather | solution.py:210
  40.4 1.3 copy-done.5
  41.8 2.9 %copy.102 = bf16[1024,1024]{0,1:T(8,128)(2,1)S(1)} copy(bf16[1024,1024]{1,0:T(8,128)(2,1)} %get-tuple-element.42) | data formatting | bytes 4194304
  44.6 2.6 %copy.87 = bf16[1024,4,256]{2,0,1:T(8,128)(2,1)} copy(bf16[1024,4,256]{0,2,1:T(8,128)(2,1)S(1)} %bitcast.104) | data formatting | bytes 4194304 | tf_op jit(solution)/shard_map/reshape | solution.py:209
  47.2 3.6 %gather_fusion = bf16[4,1024,256]{2,1,0:T(8,128)(2,1)} fusion(bf16[1024,4,256]{2,0,1:T(8,128)(2,1)} %copy.87, s32[1024]{0:T(1024)S(1)} %pad_clamp_fusion.1), kind=kCustom, calls=%fused_computation | custom fusion | bytes 4194320 | tf_op jit(solution)/shard_map/gather | solution.py:209
  50.8 1.9 %copy.106 = bf16[4,128,8,256]{3,2,0,1:T(8,128)(2,1)S(1)} copy(bf16[4,128,8,256]{3,2,1,0:T(8,128)(2,1)} %bitcast.105) | data formatting | bytes 4194304 | tf_op jit(solution)/shard_map/reshape | solution.py:209
  52.7 1.2 copy.93.seg_col.seg_all.t_col
  53.9 0.6 pad.28.clone
  54.6 0.7 pad.10.clone
  55.3 2.3 %fusion.14 = f32[1024,32]{1,0:T(8,128)S(1)} fusion(bf16[1024,3072]{1,0:T(8,128)(2,1)} %param.15, bf16[1024,16]{0,1:T(8,128)(2,1)S(1)} %fusion.38, bf16[1024,16]{0,1:T(8,128)(2,1)S(1)} %select_convert_fusion), kind=kOutput, calls=%fused_computation.18 | convolution fusion | flops 67239936 | bytes 2293760 | tf_op jit(solution)/shard_map/dot_general | solution.py:215
  58.3 0.8 subtract_convert_fusion
  59.1 0.9 slice_multiply_fusion.1
  60.0 3.6 %concatenate.49.weights = bf16[1024,640]{1,0:T(8,128)(2,1)} concatenate(bf16[1024,256]{1,0:T(8,128)(2,1)} %slice_multiply_fusion.1, bf16[1024,256]{1,0:T(8,128)(2,1)S(1)} %slice.260, bf16[1024,4]{1,0:T(8,128)(2,1)} %get-tuple-element.40, bf16[1024,4]{1,0:T(8,128)(2,1)S(1)} %broadcast_in_dim.42, bf16[1024,4]{1,0:T(8,128)(2,1)S(1)} %get-tuple-element.39, ...), dimensions={1} | concatenate | bytes 2621440 | tf_op jit(solution)/shard_map/concatenate | solution.py:222
  64.2 3.2 %pad_maximum_fusion.x = bf16[1024,1152]{1,0:T(8,128)(2,1)} fusion(bf16[256,1152]{1,0:T(8,128)(2,1)} %collective-permute-done.2, bf16[256,1152]{1,0:T(8,128)(2,1)} %collective-permute-done.1, bf16[256,1152]{1,0:T(8,128)(2,1)} %collective-permute-done, bf16[256,1152]{1,0:T(8,128)(2,1)} %bitcast.3), kind=kLoop, calls=%fused_computation.5 | loop fusion | flops 9437184 | bytes 4718592 | tf_op jit(solution)/shard_map/concatenate | solution.py:243
  67.5 5.1 %shard_map.114 = (bf16[1024,512]{1,0:T(8,128)(2,1)}, f32[1024,128]{1,0:T(8,128)}) custom-call(bf16[1024,1152]{1,0:T(8,128)(2,1)} %pad_maximum_fusion.x, bf16[1024,640]{1,0:T(8,128)(2,1)} %concatenate.49.weights), custom_call_target="tpu_custom_call" | custom-call | tf_op jit(solution)/shard_map/pallas_call | solution.py:244
  72.5 12.3 %shard_map.115 = (f32[1024,256]{1,0:T(8,128)}, bf16[4,1024,1024]{2,1,0:T(8,128)(2,1)}, f32[1024,128]{1,0:T(8,128)}, f32[8,1024]{1,0:T(8,128)}) custom-call(bf16[1024,512]{1,0:T(8,128)(2,1)} %get-tuple-element.17.query.key, bf16[1024,512]{1,0:T(8,128)(2,1)} %get-tuple-element.17.query.key, f32[1024,128]{1,0:T(8,128)} %get-tuple-element.18.z, ...), custom_call_target="tpu_custom_call" | custom-call | tf_op jit(solution)/shard_map/pallas_call | solution.py:267
  84.9 1.4 slice_reduce_fusion
  86.5 1.3 convert_element_type.138
  88.9 0.8 fusion.80
  89.8 1.5 collective-permute-start.6
  91.3 1.1 copy.111
  92.4 1.0 copy.113
  93.4 3.6 %fusion.72 = (f32[1024]{0:T(1024)}, f32[1024]{0:T(1024)S(1)}, f32[1024,1]{1,0:T(8,128)}, f32[1024,1]{1,0:T(8,128)}) fusion(f32[1024,4]{1,0:T(8,128)S(1)} %slice_convert_fusion.3, f32[1,1024]{0,1:T(8,128)} %copy.113, f32[1,1024]{0,1:T(8,128)} %copy.111, f32[1024,128]{1,0:T(8,128)} %get-tuple-element.20.stat), kind=kLoop, calls=%fused_computation.142 | loop fusion | flops 6144 | bytes 45056 | tf_op jit(solution)/shard_map/exp2 | solution.py:303
  97.7 11.1 %shard_map.116 = (bf16[256,1024]{1,0:T(8,128)(2,1)}, f32[8,1024]{1,0:T(8,128)}, bf16[1024,256]{1,0:T(8,128)(2,1)}, f32[1024,1]{1,0:T(8,128)}) custom-call(bf16[4,1024,1024]{2,1,0:T(8,128)(2,1)} %get-tuple-element.19.e, f32[1024,128]{1,0:T(8,128)} %get-tuple-element.20.stat, bf16[1024,512]{1,0:T(8,128)(2,1)} %get-tuple-element.17.query.key, ...), custom_call_target="tpu_custom_call" | custom-call | tf_op jit(solution)/shard_map/pallas_call | solution.py:309
  108.7 0.8 subtract_convert_fusion.2
  109.6 1.9 %fusion.2 = f32[272,1024]{1,0:T(8,128)S(1)} fusion(bf16[1024,1152]{1,0:T(8,128)(2,1)S(1)} %copy-done.2, bf16[4,1024]{1,0:T(4,128)(2,1)S(1)} %get-tuple-element.37, bf16[4,1024]{1,0:T(4,128)(2,1)S(1)} %get-tuple-element.38, bf16[256,1024]{1,0:T(8,128)(2,1)} %get-tuple-element.24, bf16[272]{0:T(512)(128)(2,1)S(1)} %copy-done.18), kind=kOutput, calls=%fused_computation.9 | convolution fusion | flops 572653568 | bytes 3752960 | tf_op jit(solution)/shard_map/dot_general | solution.py:358
  111.7 1.0 maximum_maximum_fusion.1
  112.6 0.7 slice.218
  113.3 0.7 fusion.11
  114.2 1.2 fusion.36
  115.6 1.3 maximum_maximum_fusion
  116.8 3.8 %all-to-all-start.2 = ((bf16[8,528,128]{2,1,0:T(8,128)(2,1)}), bf16[8,528,128]{2,1,0:T(8,128)(2,1)S(1)}, u32[]{:S(2)}, u32[]{:S(2)}) async-start(bf16[8,528,128]{2,1,0:T(8,128)(2,1)} %maximum_maximum_fusion), calls=%async_computation.2 | async-start | bytes 2162688 | tf_op jit(solution)/shard_map/all_to_all | solution.py:382
  121.3 1.3 collective-permute-start.10
  122.6 1.6 fusion.79
  124.1 0.7 convert_add_fusion.5
  125.4 2.0 %collective-permute-done.9 = bf16[272,256]{1,0:T(8,128)(2,1)S(1)} collective-permute-done((bf16[272,256]{1,0:T(8,128)(2,1)S(1)}, bf16[272,256]{1,0:T(8,128)(2,1)S(1)}, u32[]{:S(2)}, u32[]{:S(2)}) %collective-permute-start.9) | collective-permute-done | bytes 139296 | tf_op jit(solution)/shard_map/ppermute | solution.py:193
  127.4 1.9 %collective-permute-done.10 = bf16[272,256]{1,0:T(8,128)(2,1)S(1)} collective-permute-done((bf16[272,256]{1,0:T(8,128)(2,1)S(1)}, bf16[272,256]{1,0:T(8,128)(2,1)S(1)}, u32[]{:S(2)}, u32[]{:S(2)}) %collective-permute-start.10) | collective-permute-done | bytes 139296 | tf_op jit(solution)/shard_map/ppermute | solution.py:193
  129.3 2.5 %fusion.27 = f32[256,1024]{1,0:T(8,128)S(1)} fusion(bf16[1024,1024]{1,0:T(8,128)(2,1)} %bitcast.107, bf16[256,256]{1,0:T(8,128)(2,1)S(1)} %slice.284, bf16[256,256]{1,0:T(8,128)(2,1)S(1)} %slice.282, bf16[256,256]{1,0:T(8,128)(2,1)S(1)} %slice.280, bf16[256,256]{1,0:T(8,128)(2,1)S(1)} %copy-done.11), kind=kOutput, calls=%fused_computation.44 | convolution fusion | flops 538968064 | bytes 3670016 | tf_op jit(solution)/shard_map/dr,ed->re/dot_general | solution.py:416
  131.8 1.0 fusion.42
  132.9 2.8 %fusion.7.normed_grad = f32[256,1024]{1,0:T(8,128)} fusion(f32[256,1024]{1,0:T(8,128)S(1)} %fusion.42, f32[256,1024]{1,0:T(8,128)S(1)} %fusion.27, bf16[1024,1024]{1,0:T(8,128)(2,1)S(1)} %bitcast.101, bf16[256,256]{1,0:T(8,128)(2,1)S(1)} %collective-permute-done.7, bf16[256,256]{1,0:T(8,128)(2,1)} %collective-permute-done.6, ...), kind=kOutput, calls=%fused_computation.15 | convolution fusion | flops 539754496 | bytes 5768192 | tf_op jit(solution)/shard_map/rd,ed->re/dot_general | solution.py:415
  135.7 2.7 %shard_map.117 = bf16[8,32,1024]{2,1,0:T(8,128)(2,1)} custom-call(s32[1,8]{1,0:T(1,128)} %source.3, f32[256,1024]{1,0:T(8,128)} %fusion.7.normed_grad, bf16[8,32,1024]{2,1,0:T(8,128)(2,1)} %get-tuple-element.26.rows, f32[8,32,1]{2,1,0:T(8,128)} %get-tuple-element.27.inverse, f32[256,1]{1,0:T(8,128)} %get-tuple-element.50.grad, f32[1,1024]{1,0:T(1,128)} %bitcast.130, ...), custom_call_target="tpu_custom_call" | custom-call | tf_op jit(solution)/shard_map/pallas_call | solution.py:420
  138.4 9.1 %all-to-all-done.2 = bf16[8,528,128]{2,1,0:T(8,128)(2,1)S(1)} async-done(((bf16[8,528,128]{2,1,0:T(8,128)(2,1)}), bf16[8,528,128]{2,1,0:T(8,128)(2,1)S(1)}, u32[]{:S(2)}, u32[]{:S(2)}) %all-to-all-start.2) | async-done | bytes 1081376 | tf_op jit(solution)/shard_map/all_to_all | solution.py:382
  147.5 3.6 %all-to-all-start.1 = ((bf16[8,32,1024]{2,1,0:T(8,128)(2,1)}), bf16[8,32,1024]{2,1,0:T(8,128)(2,1)S(1)}, u32[]{:S(2)}, u32[]{:S(2)}) async-start(bf16[8,32,1024]{2,1,0:T(8,128)(2,1)} %shard_map.117), calls=%async_computation.1 | async-start | bytes 1048576 | tf_op jit(solution)/shard_map/all_to_all | solution.py:425
  151.9 4.7 %collective-permute-done.12 = bf16[524,128]{1,0:T(8,128)(2,1)S(1)} collective-permute-done((bf16[524,128]{1,0:T(8,128)(2,1)S(1)}, bf16[524,128]{1,0:T(8,128)(2,1)S(1)}, u32[]{:S(2)}, u32[]{:S(2)}) %collective-permute-start.12) | collective-permute-done | bytes 134176 | tf_op jit(solution)/shard_map/ppermute | solution.py:193
  156.7 0.8 dynamic_slice.17
  157.4 8.3 %all-to-all-done.1 = bf16[8,32,1024]{2,1,0:T(8,128)(2,1)S(1)} async-done(((bf16[8,32,1024]{2,1,0:T(8,128)(2,1)}), bf16[8,32,1024]{2,1,0:T(8,128)(2,1)S(1)}, u32[]{:S(2)}, u32[]{:S(2)}) %all-to-all-start.1) | async-done | bytes 524320 | tf_op jit(solution)/shard_map/all_to_all | solution.py:425
  165.7 1.4 gather_fusion.2
  167.2 0.9 gather_fusion.3
  168.4 0.7 dynamic-slice_bitcast_fusion
  169.1 3.6 %all-to-all-start.3 = ((bf16[8,96,128]{2,1,0:T(8,128)(2,1)}), bf16[8,96,128]{2,1,0:T(8,128)(2,1)S(1)}, u32[]{:S(2)}, u32[]{:S(2)}) async-start(bf16[8,96,128]{2,1,0:T(8,128)(2,1)} %dynamic-slice_bitcast_fusion), calls=%async_computation.3 | async-start | bytes 393216 | tf_op jit(solution)/shard_map/all_to_all | solution.py:408
  172.8 0.7 broadcast_multiply_fusion
  173.5 7.4 %all-to-all-done.3 = bf16[8,96,128]{2,1,0:T(8,128)(2,1)S(1)} async-done(((bf16[8,96,128]{2,1,0:T(8,128)(2,1)}), bf16[8,96,128]{2,1,0:T(8,128)(2,1)S(1)}, u32[]{:S(2)}, u32[]{:S(2)}) %all-to-all-start.3) | async-done | bytes 196640 | tf_op jit(solution)/shard_map/all_to_all | solution.py:408
  180.9 0.8 copy_bitcast_fusion.2
  (122 shorter events, 8.1 us)
Async XLA Ops:
  0.6 11.2 %copy-start = (s32[8,3]{0,1:T(4,128)S(1)}, s32[8,3]{0,1:T(4,128)}, u32[]{:S(2)}) copy-start(s32[8,3]{0,1:T(4,128)} %param.13) | copy-start | bytes 292
  0.6 11.7 %copy-start.7 = (bf16[1024,1024]{1,0:T(8,128)(2,1)S(1)}, bf16[1024,1024]{1,0:T(8,128)(2,1)}, u32[]{:S(2)}) copy-start(bf16[1024,1024]{1,0:T(8,128)(2,1)} %param.16) | copy-start | bytes 6291460
  0.7 11.7 %copy-start.15 = (f32[1024]{0:T(1024)S(1)}, f32[1024]{0:T(1024)}, u32[]{:S(2)}) copy-start(f32[1024]{0:T(1024)} %param.17) | copy-start | bytes 12292
  4.4 23.2 %all-to-all-start = ((bf16[8,32,1152]{2,1,0:T(8,128)(2,1)}), bf16[8,32,1152]{2,1,0:T(8,128)(2,1)S(1)}, u32[]{:S(2)}, u32[]{:S(2)}) async-start(bf16[8,32,1152]{2,1,0:T(8,128)(2,1)} %shard_map.112), calls=%async_computation | async-start | bytes 1179648 | tf_op jit(solution)/shard_map/all_to_all | solution.py:233
  12.4 40.3 %copy-start.14 = (s32[1024]{0:T(1024)}, s32[1024]{0:T(1024)S(1)}, u32[]{:S(2)}) copy-start(s32[1024]{0:T(1024)S(1)} %convert_reduce_fusion.1) | copy-start | bytes 12292
  27.5 0.8 copy-start.6
  30.8 27.0 %collective-permute-start.1 = (bf16[256,1152]{1,0:T(8,128)(2,1)}, bf16[256,1152]{1,0:T(8,128)(2,1)}, u32[]{:S(2)}, u32[]{:S(2)}) collective-permute-start(bf16[256,1152]{1,0:T(8,128)(2,1)} %bitcast.3), channel_id=1, source_target_pairs={{0,2},{1,3},{2,0},{3,1},{4,6},{5,7},{6,4},{7,5},{8,10},{9,11},{10,... | collective-permute-start | bytes 1769480 | tf_op jit(solution)/shard_map/ppermute | solution.py:193
  32.4 14.9 %copy-start.17 = (s32[1024]{0:T(1024)}, s32[1024]{0:T(1024)S(1)}, u32[]{:S(2)}) copy-start(s32[1024]{0:T(1024)S(1)} %pad_clamp_fusion.1) | copy-start | bytes 12292
  40.4 1.4 copy-start.5
  52.7 6.4 %copy-start.3 = (bf16[4,128,8,256]{3,2,0,1:T(8,128)(2,1)}, bf16[4,128,8,256]{3,2,0,1:T(8,128)(2,1)S(1)}, u32[]{:S(2)}) copy-start(bf16[4,128,8,256]{3,2,0,1:T(8,128)(2,1)S(1)} %copy.106) | copy-start | bytes 6291460
  57.7 6.5 %collective-permute-start = (bf16[256,1152]{1,0:T(8,128)(2,1)}, bf16[256,1152]{1,0:T(8,128)(2,1)}, u32[]{:S(2)}, u32[]{:S(2)}) collective-permute-start(bf16[256,1152]{1,0:T(8,128)(2,1)} %bitcast.3), channel_id=1, source_target_pairs={{0,1},{1,0},{2,3},{3,2},{4,5},{5,4},{6,7},{7,6},{8,9},{9,8},{10,11... | collective-permute-start | bytes 1769480 | tf_op jit(solution)/shard_map/ppermute | solution.py:193
  57.8 6.4 %collective-permute-start.2 = (bf16[256,1152]{1,0:T(8,128)(2,1)}, bf16[256,1152]{1,0:T(8,128)(2,1)}, u32[]{:S(2)}, u32[]{:S(2)}) collective-permute-start(bf16[256,1152]{1,0:T(8,128)(2,1)} %collective-permute-done.1), channel_id=1, source_target_pairs={{0,1},{1,0},{2,3},{3,2},{4,5},{5,4},{6,7},{7,6},{8,9},{9,8},{10,11... | collective-permute-start | bytes 1769480 | tf_op jit(solution)/shard_map/ppermute | solution.py:193
  72.5 13.9 %copy-start.2 = (bf16[1024,1152]{1,0:T(8,128)(2,1)S(1)}, bf16[1024,1152]{1,0:T(8,128)(2,1)}, u32[]{:S(2)}) copy-start(bf16[1024,1152]{1,0:T(8,128)(2,1)} %pad_maximum_fusion.x) | copy-start | bytes 7077892
  86.3 1.5 collective-permute-start.3
  88.4 4.0 %collective-permute-start.4 = (f32[4,256]{1,0:T(4,128)}, f32[4,256]{1,0:T(4,128)S(1)}, u32[]{:S(2)}, u32[]{:S(2)}) collective-permute-start(f32[4,256]{1,0:T(4,128)} %get-tuple-element.59), channel_id=1, source_target_pairs={{0,2},{1,3},{2,0},{3,1},{4,6},{5,7},{6,4},{7,5},{8,10},{9,11},{10,... | collective-permute-start | bytes 12296 | tf_op jit(solution)/shard_map/ppermute | solution.py:193
  89.6 43.2 %collective-permute-start.5 = (bf16[256,256]{1,0:T(8,128)(2,1)}, bf16[256,256]{1,0:T(8,128)(2,1)}, u32[]{:S(2)}, u32[]{:S(2)}) collective-permute-start(bf16[256,256]{1,0:T(8,128)(2,1)} %get-tuple-element.55), channel_id=1, source_target_pairs={{0,1},{1,0},{2,3},{3,2},{4,5},{5,4},{6,7},{7,6},{8,9},{9,8},{10,11... | collective-permute-start | bytes 393224 | tf_op jit(solution)/shard_map/ppermute | solution.py:193
  89.8 43.1 %collective-permute-start.6 = (bf16[256,256]{1,0:T(8,128)(2,1)}, bf16[256,256]{1,0:T(8,128)(2,1)}, u32[]{:S(2)}, u32[]{:S(2)}) collective-permute-start(bf16[256,256]{1,0:T(8,128)(2,1)} %get-tuple-element.54), channel_id=1, source_target_pairs={{0,2},{1,3},{2,0},{3,1},{4,6},{5,7},{6,4},{7,5},{8,10},{9,11},{10,... | collective-permute-start | bytes 393224 | tf_op jit(solution)/shard_map/ppermute | solution.py:193
  97.7 11.9 %copy-start.18 = (bf16[272]{0:T(512)(128)(2,1)S(1)}, bf16[272]{0:T(512)(128)(2,1)}, u32[]{:S(2)}) copy-start(bf16[272]{0:T(512)(128)(2,1)} %pad.28.clone) | copy-start | bytes 1636
  109.6 2.0 %copy-start.13 = (bf16[4,1024]{1,0:T(4,128)(2,1)}, bf16[4,1024]{1,0:T(4,128)(2,1)S(1)}, u32[]{:S(2)}) copy-start(bf16[4,1024]{1,0:T(4,128)(2,1)S(1)} %get-tuple-element.38) | copy-start | bytes 24580
  109.6 2.0 %copy-start.9 = (bf16[256,1024]{1,0:T(8,128)(2,1)S(1)}, bf16[256,1024]{1,0:T(8,128)(2,1)}, u32[]{:S(2)}) copy-start(bf16[256,1024]{1,0:T(8,128)(2,1)} %get-tuple-element.24) | copy-start | bytes 1572868
  111.5 1.8 copy-start.10
  113.3 2.1 %copy-start.19 = (s32[256]{0:T(256)S(1)}, s32[256]{0:T(256)}, u32[]{:S(2)}) copy-start(s32[256]{0:T(256)} %and_select_fusion) | copy-start | bytes 3076
  114.0 1.5 copy-start.16
  115.6 5.1 %copy-start.8 = (bf16[272,1024]{1,0:T(8,128)(2,1)S(1)}, bf16[272,1024]{1,0:T(8,128)(2,1)}, u32[]{:S(2)}) copy-start(bf16[272,1024]{1,0:T(8,128)(2,1)} %maximum_maximum_fusion.1) | copy-start | bytes 1671172
  116.8 8.0 %copy-start.12 = (bf16[256,256]{1,0:T(8,128)(2,1)S(1)}, bf16[256,256]{1,0:T(8,128)(2,1)}, u32[]{:S(2)}) copy-start(bf16[256,256]{1,0:T(8,128)(2,1)} %get-tuple-element.53) | copy-start | bytes 393220
  116.8 12.5 %copy-start.11 = (bf16[256,256]{1,0:T(8,128)(2,1)S(1)}, bf16[256,256]{1,0:T(8,128)(2,1)}, u32[]{:S(2)}) copy-start(bf16[256,256]{1,0:T(8,128)(2,1)} %slice.218) | copy-start | bytes 393220
  116.8 30.6 %all-to-all-start.2 = ((bf16[8,528,128]{2,1,0:T(8,128)(2,1)}), bf16[8,528,128]{2,1,0:T(8,128)(2,1)S(1)}, u32[]{:S(2)}, u32[]{:S(2)}) async-start(bf16[8,528,128]{2,1,0:T(8,128)(2,1)} %maximum_maximum_fusion), calls=%async_computation.2 | async-start | bytes 2162688 | tf_op jit(solution)/shard_map/all_to_all | solution.py:382
  120.7 4.2 %collective-permute-start.8 = (bf16[272,256]{1,0:T(8,128)(2,1)S(1)}, bf16[272,256]{1,0:T(8,128)(2,1)S(1)}, u32[]{:S(2)}, u32[]{:S(2)}) collective-permute-start(bf16[272,256]{1,0:T(8,128)(2,1)S(1)} %get-tuple-element.45), channel_id=1, source_target_pairs={{0,1},{1,0},{2,3},{3,2},{4,5},{5,4},{6,7},{7,6},{8,9},{9,8},{10,11... | collective-permute-start | bytes 417800 | tf_op jit(solution)/shard_map/ppermute | solution.py:193
  120.7 6.6 %collective-permute-start.9 = (bf16[272,256]{1,0:T(8,128)(2,1)S(1)}, bf16[272,256]{1,0:T(8,128)(2,1)S(1)}, u32[]{:S(2)}, u32[]{:S(2)}) collective-permute-start(bf16[272,256]{1,0:T(8,128)(2,1)S(1)} %get-tuple-element.47), channel_id=1, source_target_pairs={{0,2},{1,3},{2,0},{3,1},{4,6},{5,7},{6,4},{7,5},{8,10},{9,11},{10,... | collective-permute-start | bytes 417800 | tf_op jit(solution)/shard_map/ppermute | solution.py:193
  121.3 7.9 %collective-permute-start.10 = (bf16[272,256]{1,0:T(8,128)(2,1)S(1)}, bf16[272,256]{1,0:T(8,128)(2,1)S(1)}, u32[]{:S(2)}, u32[]{:S(2)}) collective-permute-start(bf16[272,256]{1,0:T(8,128)(2,1)S(1)} %get-tuple-element.46), channel_id=1, source_target_pairs={{0,3},{1,2},{2,1},{3,0},{4,7},{5,6},{6,5},{7,4},{8,11},{9,10},{10,... | collective-permute-start | bytes 417800 | tf_op jit(solution)/shard_map/ppermute | solution.py:193
  124.8 8.1 %collective-permute-start.7 = (bf16[256,256]{1,0:T(8,128)(2,1)S(1)}, bf16[256,256]{1,0:T(8,128)(2,1)S(1)}, u32[]{:S(2)}, u32[]{:S(2)}) collective-permute-start(bf16[256,256]{1,0:T(8,128)(2,1)S(1)} %copy-done.12), channel_id=1, source_target_pairs={{0,3},{1,2},{2,1},{3,0},{4,7},{5,6},{6,5},{7,4},{8,11},{9,10},{10,... | collective-permute-start | bytes 393224 | tf_op jit(solution)/shard_map/ppermute | solution.py:193
  129.3 3.6 %copy-start.4 = (bf16[4,128,8,256]{3,2,0,1:T(8,128)(2,1)S(1)}, bf16[4,128,8,256]{3,2,0,1:T(8,128)(2,1)}, u32[]{:S(2)}) copy-start(bf16[4,128,8,256]{3,2,0,1:T(8,128)(2,1)} %copy-done.3) | copy-start | bytes 6291460
  135.7 21.0 %copy-start.20 = (s32[1,8]{1,0:T(1,128)S(1)}, s32[1,8]{1,0:T(1,128)}, u32[]{:S(2)}) copy-start(s32[1,8]{1,0:T(1,128)} %dest.1) | copy-start | bytes 100
  147.5 18.3 %all-to-all-start.1 = ((bf16[8,32,1024]{2,1,0:T(8,128)(2,1)}), bf16[8,32,1024]{2,1,0:T(8,128)(2,1)S(1)}, u32[]{:S(2)}, u32[]{:S(2)}) async-start(bf16[8,32,1024]{2,1,0:T(8,128)(2,1)} %shard_map.117), calls=%async_computation.1 | async-start | bytes 1048576 | tf_op jit(solution)/shard_map/all_to_all | solution.py:425
  151.4 5.3 %collective-permute-start.12 = (bf16[524,128]{1,0:T(8,128)(2,1)S(1)}, bf16[524,128]{1,0:T(8,128)(2,1)S(1)}, u32[]{:S(2)}, u32[]{:S(2)}) collective-permute-start(bf16[524,128]{1,0:T(8,128)(2,1)S(1)} %concatenate.60), channel_id=1, source_target_pairs={{0,2},{1,3},{2,0},{3,1},{4,6},{5,7},{6,4},{7,5},{8,10},{9,11},{10,... | collective-permute-start | bytes 402440 | tf_op jit(solution)/shard_map/ppermute | solution.py:193
  151.9 15.2 %collective-permute-start.11 = (bf16[524,128]{1,0:T(8,128)(2,1)S(1)}, bf16[524,128]{1,0:T(8,128)(2,1)S(1)}, u32[]{:S(2)}, u32[]{:S(2)}) collective-permute-start(bf16[524,128]{1,0:T(8,128)(2,1)S(1)} %concatenate.60), channel_id=1, source_target_pairs={{0,1},{1,0},{2,3},{3,2},{4,5},{5,4},{6,7},{7,6},{8,9},{9,8},{10,11... | collective-permute-start | bytes 402440 | tf_op jit(solution)/shard_map/ppermute | solution.py:193
  156.6 10.5 %collective-permute-start.13 = (bf16[524,128]{1,0:T(8,128)(2,1)S(1)}, bf16[524,128]{1,0:T(8,128)(2,1)S(1)}, u32[]{:S(2)}, u32[]{:S(2)}) collective-permute-start(bf16[524,128]{1,0:T(8,128)(2,1)S(1)} %collective-permute-done.12), channel_id=1, source_target_pairs={{0,1},{1,0},{2,3},{3,2},{4,5},{5,4},{6,7},{7,6},{8,9},{9,8},{10,11... | collective-permute-start | bytes 402440 | tf_op jit(solution)/shard_map/ppermute | solution.py:193
  167.2 14.5 %copy-start.1 = (s32[8,3]{0,1:T(4,128)S(1)}, s32[8,3]{0,1:T(4,128)}, u32[]{:S(2)}) copy-start(s32[8,3]{0,1:T(4,128)} %param.13) | copy-start | bytes 292
  169.1 11.8 %all-to-all-start.3 = ((bf16[8,96,128]{2,1,0:T(8,128)(2,1)}), bf16[8,96,128]{2,1,0:T(8,128)(2,1)S(1)}, u32[]{:S(2)}, u32[]{:S(2)}) async-start(bf16[8,96,128]{2,1,0:T(8,128)(2,1)} %dynamic-slice_bitcast_fusion), calls=%async_computation.3 | async-start | bytes 393216 | tf_op jit(solution)/shard_map/all_to_all | solution.py:408

commit v2 on v0

v2 whole, which is shorter than its diff:
```python
import jax
import jax.numpy as jnp
from jax import lax
from jax.experimental import pallas as pl
from jax.experimental.pallas import tpu as pltpu
from jax.sharding import PartitionSpec as P


HEADS = 16
LANES = 128
epsilon = 1e-06
loss_scale = 64.0
log2e = 1.4426950408889634
far = 2.0**100
bf16 = jnp.bfloat16
f32 = jnp.float32


def vmem():
    return pl.BlockSpec(memory_space=pltpu.VMEM)


def smem():
    return pl.BlockSpec(memory_space=pltpu.SMEM)


def whole(shape):
    return pl.BlockSpec(shape, lambda *_: (0,) * len(shape))


def call(kernel, shapes, specs, work=0, room=8, **more):
    params = pltpu.CompilerParams(vmem_limit_bytes=room * 2**20)
    cost = pl.CostEstimate(flops=work, transcendentals=0, bytes_accessed=0)
    return pl.pallas_call(
        kernel, out_shape=shapes, in_specs=specs, compiler_params=params, cost_estimate=cost, **more
    )


def indexed(kernel, shapes, specs, out_specs, grid, scratch=(), work=0, room=8):
    params = pltpu.CompilerParams(vmem_limit_bytes=room * 2**20)
    cost = pl.CostEstimate(flops=work, transcendentals=0, bytes_accessed=0)
    spec = pltpu.PrefetchScalarGridSpec(
        num_scalar_prefetch=1, grid=grid, in_specs=specs, out_specs=out_specs, scratch_shapes=scratch
    )
    return pl.pallas_call(
        kernel, out_shape=shapes, grid_spec=spec, compiler_params=params, cost_estimate=cost
    )


def near(values):
    return pltpu.with_memory_space_constraint(values, pltpu.VMEM)


def stay(values):
    return pltpu.with_memory_space_constraint(values, pltpu.HBM)


def contract(left, right, dims, **more):
    return lax.dot_general(left, right, (dims, ((), ())), preferred_element_type=f32, **more)


def prepare_kernel(w_v, w_out, score, u_out, turned_out, proj_out):
    width = w_v.shape[0]
    half = LANES // 2
    u = jnp.sum(w_out[...].astype(f32) * score[...], axis=1, keepdims=True)
    u_out[...] = u
    high = u.astype(bf16).astype(f32)
    lane = lax.broadcasted_iota(jnp.int32, (width, LANES), 1)
    head = lax.broadcasted_iota(jnp.int32, (width, LANES), 0) // (width // HEADS)
    columns = jnp.where(lane == head, high, 0.0)
    columns = jnp.where(lane == half + head, u - high, columns).astype(bf16)
    g = jnp.dot(w_v[...], columns, preferred_element_type=f32)
    g = g + pltpu.roll(g, half, axis=1)
    high = g.astype(bf16).astype(f32)
    tops, rests = high.T[:HEADS], (g - high).T[:HEADS]
    turned_out[...] = jnp.concatenate([tops, tops, rests], axis=0).astype(bf16)
    proj_out[...] = jnp.where(lane < half, high, g - high).astype(bf16)


def pack_kernel(dest, rows, grades, out):
    count, piece, width = rows.shape
    total = grades.shape[1]
    row = lax.broadcasted_iota(jnp.int32, (piece, total), 0)
    lane = lax.broadcasted_iota(jnp.int32, (piece, total), 1)
    line = grades[...].astype(f32)
    for b in range(count):
        grade = jnp.sum(jnp.where(lane == row + b * piece, line, 0.0), axis=1, keepdims=True)
        out[dest[0, b], :, :width] = rows[b]
        out[dest[0, b], :, width:] = jnp.broadcast_to(grade, (piece, LANES)).astype(bf16)


def norm_kernel(source, table, incoming, gain, score, ready, out):
    count, piece, wide = incoming.shape
    width = wide - LANES
    lane = lax.broadcasted_iota(jnp.int32, (piece, LANES), 1)
    for c in range(count):
        block = incoming[source[0, c]]
        values = block[:, :width].astype(f32)
        inverse = lax.rsqrt(jnp.mean(values * values, axis=1, keepdims=True) + epsilon)
        out[c, :, :width] = (values * inverse * gain[...]).astype(bf16)
        base = jnp.sum(values * score[...], axis=1, keepdims=True)
        high = base.astype(bf16).astype(f32)
        middle = (base - high).astype(bf16).astype(f32)
        low = base - high - middle
        info = jnp.where(lane == 1, high, block[:, width:].astype(f32))
        info = jnp.where(lane == 2, middle, info)
        info = jnp.where(lane == 3, low, info)
        out[c, :, width:] = info.astype(bf16)


def list_of(table, narrow, lists, first, shape, axis):
    position = lax.broadcasted_iota(jnp.int32, shape, axis) + first
    found = jnp.zeros(shape, jnp.int32)
    for s in range(lists):
        found = found + (position >= table[narrow + s]).astype(jnp.int32)
    return found


def forward_kernel(table, *refs, narrow, lists):
    blocks = refs[:narrow]
    w_q, w_k, g, k_out, e_out, q_out, x_out, stat_out, part_out, z_out, lines_out, xs, qs, kx, zt = refs[narrow:]
    local = blocks[0].shape[0]
    width = w_q.shape[0]
    heads = e_out.shape[0]
    half = LANES // 2
    scale = half**-0.5
    step = pl.program_id(0)

    @pl.when(step == 0)
    def _():
        lane = lax.broadcasted_iota(jnp.int32, (local, LANES), 1)
        for m in range(narrow):
            rows = pl.ds(m * local, local)
            block = blocks[m][:, :width]
            xs[rows, :] = blocks[m][...]
            qs[rows, :] = (jnp.dot(block, w_q[...], preferred_element_type=f32) * scale).astype(bf16)
            keys = jnp.dot(block, w_k[...], preferred_element_type=f32).astype(bf16)
            segment = list_of(table, narrow, lists, table[m] * local, (local, LANES), 0)
            away = jnp.where(lane == segment, 0.0, -far).astype(bf16)
            for p in range(heads // 2):
                kx[p, rows, :LANES] = keys[:, p * LANES : (p + 1) * LANES]
                kx[p, rows, LANES:] = away
            k_out[rows, :] = keys
            turned = jnp.dot(block, g[...], preferred_element_type=f32).T
            zt[:, rows] = turned[:HEADS] + turned[half : half + HEADS]
            info = blocks[m][:, width:].astype(f32).T
            lines_out[0:1, rows] = info[1:2] + info[2:3] + info[3:4]
            lines_out[1:2, rows] = jnp.exp2(info[0:1])
            lines_out[2:3, rows] = list_of(table, narrow, lists, table[m] * local, (1, local), 1).astype(f32)
        z_out[...] = zt[...]

    at = pl.ds(pl.multiple_of(step * local, local), local)
    query = qs[at, :]
    q_out[...] = query
    x_out[...] = xs[at, :]
    lane = lax.broadcasted_iota(jnp.int32, (local, LANES), 1)
    segment = list_of(table, narrow, lists, table[step] * local, (local, LANES), 0)
    mine = (lane == segment).astype(f32).astype(bf16)
    stats = jnp.zeros((local, LANES), f32)
    zsum = jnp.zeros((local, 1), f32)
    for p in range(heads // 2):
        for s in range(2):
            h = 2 * p + s
            own = query[:, p * LANES : (p + 1) * LANES]
            own = jnp.where((lane >= half) == (s == 1), own, jnp.zeros_like(own))
            logits = contract(jnp.concatenate([own, mine], axis=1), kx[p], ((1,), (1,)))
            weights = jnp.exp2(logits * log2e)
            e_out[h] = weights.astype(bf16)
            zrow = zt[pl.ds(table[0] * heads + h, 1), :]
            inverse = 1.0 / jnp.sum(weights, axis=1, keepdims=True)
            zeta = jnp.sum(weights * zrow, axis=1, keepdims=True) * inverse
            stats = jnp.where(lane == h, zeta, stats)
            stats = jnp.where(lane == heads + h, inverse, stats)
            zsum = zsum + zeta
    stat_out[...] = stats
    part_out[...] = jnp.broadcast_to(zsum, (local, LANES)).T[:1]


def center_kernel(table, e, stat, key, z, a_out):
    heads = e.shape[0]
    rows = stat.shape[0]
    half = LANES // 2
    here = pl.ds(pl.multiple_of(pl.program_id(0) * rows, rows), rows)
    lane = lax.broadcasted_iota(jnp.int32, (rows, LANES), 1)
    stats = stat[...]
    for p in range(heads // 2):
        at = slice(p * LANES, (p + 1) * LANES)
        parts = []
        for h in (2 * p, 2 * p + 1):
            zrow = z[pl.ds(table[0] * heads + h, 1), :]
            centred = (e[h, here, :].astype(f32) * (zrow - stats[:, h : h + 1])).astype(bf16)
            part = jnp.dot(centred, key[:, at], preferred_element_type=f32)
            parts.append(part * stats[:, heads + h : heads + h + 1])
        a_out[:, at] = jnp.where(lane >= half, parts[1], parts[0]).astype(bf16)


def score_kernel(table, *refs, narrow):
    partials = refs[:narrow]
    given, x, a, grad_out, gq_out, lines, acc = refs[narrow:]
    local, _ = a.shape
    width = x.shape[1] - LANES
    scale = (LANES // 2) ** -0.5
    wide, _, chunk = gq_out.shape
    step = pl.program_id(0)

    @pl.when(step == 0)
    def _():
        acc[...] = jnp.zeros_like(acc)
        lines[...] = given[...]
        for m in range(narrow):
            rows = pl.ds(m * local, local)
            summed = given[0:1, rows]
            for d in range(narrow):
                summed = summed + partials[d][:, (m ^ d) * local : ((m ^ d) + 1) * local]
            lines[0:1, rows] = summed

    at = pl.ds(pl.multiple_of(step * local, local), local)
    turned = jnp.concatenate([lines[:, at]] * (LANES // 8), axis=0).T
    same = turned[:, 2:3] == lines[2:3, :]
    gains = lines[1:2, :]
    spread = gains - turned[:, 1:2]
    margin = turned[:, 0:1] - lines[0:1, :]
    margin = jnp.where(spread > 0.0, margin, -margin)
    pulls = spread / (1.0 + jnp.exp(-margin))
    pulls = jnp.sum(jnp.where(same, pulls, 0.0), axis=1, keepdims=True)
    norm = jnp.sum(jnp.where(same, gains, 0.0), axis=1, keepdims=True)
    grad = loss_scale * pulls / norm
    grad_out[...] = grad
    query = (a[...].astype(f32) * (grad * scale)).astype(bf16)
    acc[...] += contract(query, x[:, :width], ((0,), (0,)))

    @pl.when(step == pl.num_programs(0) - 1)
    def _():
        for w in range(wide):
            gq_out[w] = acc[:, w * chunk : (w + 1) * chunk].astype(bf16)


def key_kernel(table, e, stat, query, z, grad, w_v, x_hbm, keys_out, keep_out, send_out, x, key_acc, c_acc, sem, at_wide):
    heads, total, _ = e.shape
    rows = query.shape[0]
    half = LANES // 2
    own = query.shape[1]
    width = w_v.shape[0]
    pairs, lines, chunk = keep_out.shape
    step = pl.program_id(0)
    copy = pltpu.make_async_copy(x_hbm, x, sem)

    @pl.when(step == 0)
    def _():
        copy.start()
        key_acc[...] = jnp.zeros_like(key_acc)
        c_acc[...] = jnp.zeros_like(c_acc)

    lane = lax.broadcasted_iota(jnp.int32, (rows, LANES), 1)
    stats = stat[...]
    here = pl.ds(pl.multiple_of(step * rows, rows), rows)
    for h in range(heads):
        p, s = h // 2, h % 2
        zeta = stats[:, h : h + 1]
        scaled = e[h, here, :].astype(f32) * (stats[:, heads + h : heads + h + 1] * grad[...])
        c_acc[h : h + 1, :] += jnp.sum(scaled, axis=0, keepdims=True)
        centred = (scaled * (z[pl.ds(table[0] * heads + h, 1), :] - zeta)).astype(bf16)
        head = query[:, p * LANES : (p + 1) * LANES]
        head = jnp.where((lane >= half) == (s == 1), head, jnp.zeros_like(head))
        key_acc[p * LANES : (p + 1) * LANES, :] += contract(head, centred, ((0,), (0,)))

    @pl.when(step == pl.num_programs(0) - 1)
    def _():
        copy.wait()
        c = c_acc[...]
        high = c.astype(bf16).astype(f32)
        parts = jnp.concatenate([high[:heads], (c - high)[:heads]], axis=0)
        extra = keys_out.shape[0] - own - 2 * heads
        parts = jnp.concatenate([parts, jnp.zeros((extra, total), f32)], axis=0)
        keys_out[:own] = key_acc[...].astype(bf16)
        keys_out[own:] = parts.astype(bf16)
        out = jnp.dot(keys_out[...], x[:, :width], preferred_element_type=f32)
        mass = out[own : own + heads] + out[own + heads : own + 2 * heads]
        high = mass.astype(bf16).astype(f32)
        tops = jnp.concatenate([high, mass - high], axis=0)
        values = jnp.dot(tops.astype(bf16), w_v[...], preferred_element_type=f32)
        values = values[:heads] + values[heads:]
        head = lax.broadcasted_iota(jnp.int32, (heads, own), 1) // half
        index = lax.broadcasted_iota(jnp.int32, (heads, own), 0)
        value = jnp.sum(jnp.where(head == index, values, 0.0), axis=0, keepdims=True)
        count = own // chunk
        cuts = [value[:, t * chunk : (t + 1) * chunk] for t in range(count)]
        fill = lines - own - heads - count
        cuts.append(jnp.zeros((fill, chunk), f32))
        wide_index = table[at_wide]
        odd = wide_index % 2 == 1

        def block(w):
            at = slice(w * chunk, (w + 1) * chunk)
            return out[:own, at], jnp.concatenate([mass[:, at]] + cuts, axis=0)

        for t in range(pairs):
            even, other = block(2 * t), block(2 * t + 1)
            place = jnp.bitwise_xor(t, wide_index // 2)
            for target, first in ((keep_out, False), (send_out, True)):
                top = jnp.where(odd != first, other[0], even[0])
                rest = jnp.where(odd != first, other[1], even[1])
                target[place, :own] = top.astype(bf16)
                target[place, own:] = rest.astype(bf16)


def query_rows_kernel(table, *refs, narrow):
    blocks = refs[:narrow]
    w_q, out = refs[narrow:]
    step = pl.program_id(0)
    for m in range(narrow):

        @pl.when(step == m)
        def _():
            term = contract(blocks[m][...], w_q[...], ((1,), (1,)))
            out[...] = term if m == 0 else out[...] + term


def tail_kernel(table, *refs, narrow, heads):
    keys = refs[:narrow]
    w_k, query_rows, turned, source, incoming, grad, gain, score, out, acc, cs = refs[narrow:]
    own = w_k.shape[1]
    count, piece, width = out.shape
    scale = (LANES // 2) ** -0.5
    step = pl.program_id(0)
    for m in range(narrow):

        @pl.when(step == m)
        def _():
            term = contract(keys[m][:own], w_k[...], ((0,), (1,)))
            acc[...] = term if m == 0 else acc[...] + term
            mass = keys[m][own:].astype(f32)
            for h in range(heads):
                cs[pl.ds(table[m] * heads + h, 1), :] = mass[h : h + 1] + mass[heads + h : heads + h + 1]

    @pl.when(step == narrow - 1)
    def _():
        mass = cs[...]
        high = mass.astype(bf16).astype(f32)
        mass = jnp.concatenate([high, mass - high, high], axis=0).astype(bf16)
        values_part = contract(mass, turned[...], ((0,), (0,)))
        acc[...] += values_part + query_rows[...] * (grad[...] * scale)
        for c in range(count):
            part = pl.ds(c * piece, piece)
            scaled = acc[part, :] * gain[...]
            values = incoming[source[0, c], :, :width].astype(f32)
            inv = lax.rsqrt(jnp.mean(values * values, axis=1, keepdims=True) + epsilon)
            mean = jnp.mean(scaled * values, axis=1, keepdims=True)
            sums = grad[part, :] * score[...] + inv * scaled - values * (inv * inv * inv * mean)
            out[source[0, c]] = sums.astype(bf16)


def body(rows, grades, block_dest, block_source, lengths, gain, w_qkv, w_out, w_score):
    wide = lax.axis_size("wide")
    narrow = lax.axis_size("narrow")
    wide_index = lax.axis_index("wide")
    narrow_index = lax.axis_index("narrow")
    local, width = rows.shape
    lists = lengths.shape[1]
    piece = local // wide
    head_size = width // HEADS
    heads = HEADS // narrow
    own = heads * head_size
    total = local * narrow
    chunk = width // wide
    order = jnp.bitwise_xor(narrow_index, jnp.arange(narrow, dtype=jnp.int32))
    bounds = jnp.cumsum(lax.dynamic_index_in_dim(lengths, wide_index, 0, keepdims=False))
    table = jnp.concatenate([order, bounds.astype(jnp.int32), wide_index[None].astype(jnp.int32)])
    gain_row, score_row = gain[None, :], w_score[None, :]

    def swap(values, m):
        return lax.ppermute(values, "narrow", [(i, i ^ m) for i in range(narrow)])

    def across(values):
        return lax.all_to_all(values, "wide", split_axis=0, concat_axis=0, tiled=True)

    def spread(values):
        held = [values] + [None] * (narrow - 1)
        for m in range(1, narrow):
            top = 1 << (m.bit_length() - 1)
            held[m] = swap(held[m ^ top], top) if m == top else None
        for m in range(1, narrow):
            if held[m] is None:
                top = 1 << (m.bit_length() - 1)
                held[m] = swap(held[top], m ^ top)
        return held

    def shape(*dims, dtype=f32):
        return jax.ShapeDtypeStruct(dims, dtype)

    w_qkv = stay(w_qkv)

    outgoing = call(
        pack_kernel, shape(wide, piece, width + LANES, dtype=bf16), [smem(), vmem(), vmem()]
    )(block_dest, stay(rows.reshape(wide, piece, width)), stay(grades[None, :]))
    incoming = across(outgoing)

    u, g_turned, g_proj = call(
        prepare_kernel,
        (shape(width, 1), shape(3 * HEADS, width, dtype=bf16), shape(width, LANES, dtype=bf16)),
        [pl.BlockSpec((width, width), lambda i: (0, 2)), whole((width, width)), whole((1, width))],
        work=10**9,
        room=24,
        grid=(1,),
        out_specs=(whole((width, 1)), whole((3 * HEADS, width)), whole((width, LANES))),
    )(w_qkv, w_out, score_row)

    normx = call(
        norm_kernel,
        shape(wide, piece, width + LANES, dtype=bf16),
        [smem(), smem(), vmem(), vmem(), vmem(), pl.BlockSpec(memory_space=pl.ANY)],
    )(block_source, table[None, :], near(incoming), gain_row, score_row, g_proj)
    blocks = spread(normx.reshape(local, width + LANES))

    row_block = lambda columns: pl.BlockSpec((local, columns), lambda i, t: (i, 0))
    key, e, queries, x, stat, part, z, lines = indexed(
        lambda *refs: forward_kernel(*refs, narrow=narrow, lists=lists),
        (
            shape(total, own, dtype=bf16),
            shape(heads, total, total, dtype=bf16),
            shape(total, own, dtype=bf16),
            shape(total, width + LANES, dtype=bf16),
            shape(total, LANES),
            shape(1, total),
            shape(HEADS, total),
            shape(8, total),
        ),
        [whole((local, width + LANES))] + [vmem()] * (narrow - 1)
        + [
            pl.BlockSpec((width, own), lambda i, t: (0, t[0])),
            pl.BlockSpec((width, own), lambda i, t: (0, narrow + t[0])),
            whole((width, LANES)),
        ],
        (
            whole((total, own)),
            pl.BlockSpec((heads, local, total), lambda i, t: (0, i, 0)),
            row_block(own),
            row_block(width + LANES),
            row_block(LANES),
            pl.BlockSpec((1, local), lambda i, t: (0, i)),
            whole((HEADS, total)),
            whole((8, total)),
        ),
        (narrow,),
        [
            pltpu.VMEM((total, width + LANES), bf16),
            pltpu.VMEM((total, own), bf16),
            pltpu.VMEM((heads // 2, total, 2 * LANES), bf16),
            pltpu.VMEM((HEADS, total), f32),
        ],
        work=4 * 10**9,
        room=28,
    )(table, blocks[0], *map(near, blocks[1:]), w_qkv, w_qkv, g_proj)

    partials = [part] + [swap(part, m) for m in range(1, narrow)]
    a = indexed(
        center_kernel,
        shape(total, own, dtype=bf16),
        [vmem(), row_block(LANES), whole((total, own)), whole((HEADS, total))],
        row_block(own),
        (narrow,),
        work=2 * 10**9,
        room=10,
    )(table, near(e), stat, key, z)
    a_rows = [a[:local]] + [swap(a[m * local : (m + 1) * local], m) for m in range(1, narrow)]

    grad, gq = indexed(
        lambda *refs: score_kernel(*refs, narrow=narrow),
        (shape(total, 1), shape(wide, own, chunk, dtype=bf16)),
        [whole((1, total))] + [vmem()] * (narrow - 1) + [whole((8, total)), row_block(width + LANES), row_block(own)],
        (row_block(1), whole((wide, own, chunk))),
        (narrow,),
        [pltpu.VMEM((8, total), f32), pltpu.VMEM((own, width), f32)],
        work=2 * 10**9,
        room=14,
    )(table, partials[0], *map(near, partials[1:]), lines, x, a)
    terms_q = across(gq)

    count_v = own // chunk
    lines_k = -(-(own + heads + count_v) // 16) * 16
    lines_c = -(-(own + 2 * heads) // 16) * 16
    keys, keep, send = indexed(
        lambda *refs: key_kernel(*refs, at_wide=narrow + lists),
        (shape(lines_c, total, dtype=bf16),) + (shape(wide // 2, lines_k, chunk, dtype=bf16),) * 2,
        [
            vmem(),
            row_block(LANES),
            row_block(own),
            whole((HEADS, total)),
            row_block(1),
            pl.BlockSpec((width, own), lambda i, t: (0, 2 * narrow + t[0])),
            pl.BlockSpec(memory_space=pl.ANY),
        ],
        (whole((lines_c, total)),) + (whole((wide // 2, lines_k, chunk)),) * 2,
        (narrow,),
        [
            pltpu.VMEM((total, width + LANES), bf16),
            pltpu.VMEM((own, total), f32),
            pltpu.VMEM((8, total), f32),
            pltpu.SemaphoreType.DMA,
        ],
        work=4 * 10**9,
        room=22,
    )(table, near(e), stat, queries, z, grad, w_qkv, x)

    k_rows = [keys[:, :local]]
    k_rows += [swap(keys[:, m * local : (m + 1) * local], m) for m in range(1, narrow)]
    step = 1
    while True:
        received = lax.ppermute(send, "wide", [(i, i ^ step) for i in range(wide)])
        sum_k = keep.astype(f32) + received.astype(f32)
        step *= 2
        if step == wide:
            break
        cut = sum_k.astype(bf16).reshape(-1, 2, lines_k, chunk)
        keep, send = cut[:, 0], cut[:, 1]
    sum_k = sum_k[0].astype(bf16)

    query_rows = indexed(
        lambda *refs: query_rows_kernel(*refs, narrow=narrow),
        shape(local, width),
        [vmem()] * narrow + [pl.BlockSpec((width, own), lambda i, t: (0, t[i]))],
        whole((local, width)),
        (narrow,),
        work=10**9,
        room=8,
    )(table, *map(near, a_rows), w_qkv)
    returning = indexed(
        lambda *refs: tail_kernel(*refs, narrow=narrow, heads=heads),
        shape(wide, piece, width, dtype=bf16),
        [vmem()] * narrow
        + [
            pl.BlockSpec((width, own), lambda i, t: (0, narrow + t[i])),
            vmem(),
            whole((3 * HEADS, width)),
            smem(),
            vmem(),
            whole((local, 1)),
            whole((1, width)),
            whole((1, width)),
        ],
        whole((wide, piece, width)),
        (narrow,),
        [pltpu.VMEM((local, width), f32), pltpu.VMEM((HEADS, local), f32)],
        work=10**9,
        room=10,
    )(
        table, *map(near, k_rows), w_qkv, near(query_rows), g_turned, block_source, near(incoming), grad, gain_row, score_row
    )
    arrived = across(returning)
    grad_rows = arrived[block_dest[0]].reshape(local, width)

    sum_q = jnp.sum(terms_q.astype(f32), axis=0)
    q_cols = jnp.stack(spread(sum_q.astype(bf16)))[order].reshape(width, chunk)
    gathered = jnp.stack(spread(sum_k))[order]
    k_cols = gathered[:, :own].reshape(width, chunk)
    m_all = gathered[:, own : own + heads].astype(f32)
    m_rows = jnp.broadcast_to(m_all.reshape(HEADS, 1, chunk), (HEADS, head_size, chunk))
    v_cols = (m_rows.reshape(width, chunk) * u).astype(bf16)
    v_all = gathered[:, own + heads : own + heads + count_v].astype(f32)
    v_all = v_all.reshape(width)
    columns = 3 * width // (wide * narrow)
    full = jnp.concatenate([q_cols, k_cols, v_cols], axis=0).reshape(wide, narrow, columns, chunk)
    mine = lax.dynamic_index_in_dim(full, narrow_index, 1, keepdims=False)
    parts = across(mine)
    grad_qkv = parts.astype(f32).transpose(0, 2, 1).reshape(width, columns)
    out_columns = width // (wide * narrow)
    place = (wide_index * narrow + narrow_index) * out_columns
    grad_out = v_all[:, None] * lax.dynamic_slice_in_dim(w_score, place, out_columns)[None, :]
    return (grad_rows, grad_qkv, grad_out)


def solution(mesh):
    both = ("wide", "narrow")
    placed = (P(both, None), P(both), P(both, None), P(both, None), P(), P(), P(), P(), P())
    return jax.shard_map(
        body,
        mesh=mesh,
        in_specs=placed,
        out_specs=(P(both, None), P(None, both), P(None, both)),
        check_vma=False,
    )
```

time: 510 us -> 136 us (0.27)
  waiting for transfers between devices: 278 us -> 46.3 us
  matrix products: 126 us -> 0 us
  Pallas kernels: 0 us -> 42.6 us
  local copies, waits for them, and re-layouts: 42.7 us -> 5.86 us
  blocking collectives: 20.8 us -> 0 us
  starting transfers between devices: 16.7 us -> 35.7 us
  between operations: 14.1 us -> 0.97 us
    reduce_scatter x2 -> x0, waiting for transfers between devices: 213 us -> none  [the longest x1 157 us: body(): lax.psum_scatter(qkv_part, ('wide', 'narrow'), scatter_dimension=1, tiled...]
    dot_general x64 -> x0, matrix products: 126 us -> none  [the longest x24 38.5 us: attend_probs(): jnp.einsum('hqd,hkd->hqk', query_part, key_part, preferred_element_type=j...]
    pallas_call x0 -> x9, Pallas kernels: none -> 42.6 us  [the longest x1 9.57 us: body(): indexed(lambda *refs: forward_kernel(*refs, narrow=narrow, lists=lists),...]
    all_gather x3 -> x0, waiting for transfers between devices: 28.4 us -> none  [the longest x1 28.4 us: body(): lax.all_gather(projected[:, width:], 'narrow', axis=0, tiled=True)]
    ppermute x0 -> x21, waiting for transfers between devices: none -> 22.8 us  [the longest x18 18.2 us: swap(): return lax.ppermute(values, 'narrow', [(i, i ^ m) for i in range(narrow)])]
    all_gather x4 -> x0, blocking collectives: 20.8 us -> none  [the longest x1 5.33 us: body(): lax.all_gather(totals_blocks.astype(jnp.bfloat16), 'narrow', axis=2, tile...]
    slice x8 -> x5, local copies, waits for them, and re-layouts: 21.3 us -> 0.82 us  [the longest x1 0.75 us: body(): a[m * local:(m + 1) * local]]
    ppermute x0 -> x21, starting transfers between devices: none -> 17.7 us  [the longest x18 10 us: swap(): return lax.ppermute(values, 'narrow', [(i, i ^ m) for i in range(narrow)])]
  transfers between devices with their start and end apart: 8 -> 25, of which waited for: 6 -> 9; matrix products, arithmetic and copies ran while one was open for 24% -> 5% of each run, Pallas kernels for 0% -> 12%
where the time goes in v2:
time: 136 us; the launch traced here: 135 us
  waiting for transfers between devices  46.3 us (34%)
  Pallas kernels  42.6 us (31%)
  starting transfers between devices  35.7 us (26%)
  local copies, waits for them, and re-layouts  5.86 us (4%)
  other arithmetic  3.5 us (3%)
    all_to_all x4, waiting for transfers between devices, across(): lax.all_to_all(values, 'wide', split_axis=0, concat_axis=0, tiled=True)  23.4 us
    ppermute x18, waiting for transfers between devices, swap(): return lax.ppermute(values, 'narrow', [(i, i ^ m) for i in range(narrow)])  18.2 us
    all_to_all x4, starting transfers between devices, across(): lax.all_to_all(values, 'wide', split_axis=0, concat_axis=0, tiled=True)  18.1 us
    ppermute x18, starting transfers between devices, swap(): return lax.ppermute(values, 'narrow', [(i, i ^ m) for i in range(narrow)])  10 us
    pallas_call x1, Pallas kernels, body(): indexed(lambda *refs: forward_kernel(*refs, narrow=narrow, lists=lists),...  9.57 us
    pallas_call x1, Pallas kernels, body(): indexed(lambda *refs: key_kernel(*refs, at_wide=narrow + lists), (shape(l...  8.22 us
    ppermute x3, starting transfers between devices, body(): received = lax.ppermute(send, 'wide', [(i, i ^ step) for i in range(wide)])  7.63 us
    pallas_call x1, Pallas kernels, body(): indexed(lambda *refs: score_kernel(*refs, narrow=narrow), (shape(total, 1...  5.97 us
  transfers between devices with their start and end apart: 25, of which 9 were waited for; matrix products, arithmetic and copies ran while one was open for 5% of the time, Pallas kernels for 12%

profile of v2, /device:TPU:0, one launch (start us, length us, event | category | flops | bytes accessed | tf_op | source)
XLA Modules:
  0.0 134.9 jit_solution(4946321428532495542)
XLA Ops:
  0.6 0.0 copy-start
  0.7 0.0 copy-start.7
  0.7 0.8 copy-done.7
  1.5 2.0 %shard_map.112 = bf16[8,32,1152]{2,1,0:T(8,128)(2,1)} custom-call(s32[1,8]{1,0:T(1,128)S(1)} %copy-done.7, bf16[8,32,1024]{2,1,0:T(8,128)(2,1)} %bitcast.76, s32[1,256]{1,0:T(1,128)} %bitcast.89), custom_call_target="tpu_custom_call" | custom-call | tf_op jit(solution)/shard_map/pallas_call | solution.py:393
  3.5 7.3 %all-to-all-start = ((bf16[8,32,1152]{2,1,0:T(8,128)(2,1)}), bf16[8,32,1152]{2,1,0:T(8,128)(2,1)S(1)}, u32[]{:S(2)}, u32[]{:S(2)}) async-start(bf16[8,32,1152]{2,1,0:T(8,128)(2,1)} %shard_map.112), calls=%async_computation | async-start | bytes 1179648 | tf_op jit(solution)/shard_map/all_to_all | solution.py:375
  10.8 0.2 dynamic-slice_reduce_fusion
  10.9 0.2 reduce-window.9
  11.1 0.0 copy-start.6
  11.1 2.9 %shard_map.113 = (f32[1024,1]{1,0:T(8,128)S(1)}, bf16[48,1024]{1,0:T(8,128)(2,1)S(1)}, bf16[1024,128]{1,0:T(8,128)(2,1)S(1)}) custom-call(bf16[1024,3072]{1,0:T(8,128)(2,1)} %refs_5_.5, bf16[1024,1024]{1,0:T(8,128)(2,1)S(1)} %copy-done.1, f32[1,1024]{1,0:T(1,128)S(1)} %bitcast.65), custom_call_target="tpu_custom_call" | custom-call | flops 1000000000 | tf_op jit(solution)/shard_map/pallas_call | solution.py:398
  14.0 0.7 copy-done.2
  14.7 0.1 pad_add_fusion.refs_0_.table
  14.8 11.9 %all-to-all-done.incoming.refs_9_ = bf16[8,32,1152]{2,1,0:T(8,128)(2,1)S(1)} async-done(((bf16[8,32,1152]{2,1,0:T(8,128)(2,1)}), bf16[8,32,1152]{2,1,0:T(8,128)(2,1)S(1)}, u32[]{:S(2)}, u32[]{:S(2)}) %all-to-all-start) | async-done | bytes 589856 | tf_op jit(solution)/shard_map/all_to_all | solution.py:375
  26.7 0.9 shard_map.114
  27.5 1.6 %collective-permute-start.1 = (bf16[256,1152]{1,0:T(8,128)(2,1)S(1)}, bf16[256,1152]{1,0:T(8,128)(2,1)S(1)}, u32[]{:S(2)}, u32[]{:S(2)}) collective-permute-start(bf16[256,1152]{1,0:T(8,128)(2,1)S(1)} %bitcast.62), channel_id=1, source_target_pairs={{0,2},{1,3},{2,0},{3,1},{4,6},{5,7},{6,4},{7,5},{8,10},{9,11},{10,... | collective-permute-start | bytes 1769480 | tf_op jit(solution)/shard_map/ppermute | solution.py:372
  29.1 12.1 %collective-permute-done.1.refs_3_ = bf16[256,1152]{1,0:T(8,128)(2,1)S(1)} collective-permute-done((bf16[256,1152]{1,0:T(8,128)(2,1)S(1)}, bf16[256,1152]{1,0:T(8,128)(2,1)S(1)}, u32[]{:S(2)}, u32[]{:S(2)}) %collective-permute-start.1) | collective-permute-done | bytes 589856 | tf_op jit(solution)/shard_map/ppermute | solution.py:372
  41.2 0.0 collective-permute-start.2
  41.2 0.0 collective-permute-done.refs_2_
  41.2 2.0 %collective-permute-done.2.refs_4_ = bf16[256,1152]{1,0:T(8,128)(2,1)S(1)} collective-permute-done((bf16[256,1152]{1,0:T(8,128)(2,1)S(1)}, bf16[256,1152]{1,0:T(8,128)(2,1)S(1)}, u32[]{:S(2)}, u32[]{:S(2)}) %collective-permute-start.2) | collective-permute-done | bytes 589856 | tf_op jit(solution)/shard_map/ppermute | solution.py:372
  43.2 9.6 %shard_map.115 = (bf16[1024,256]{1,0:T(8,128)(2,1)S(1)}, bf16[4,1024,1024]{2,1,0:T(8,128)(2,1)S(1)}, bf16[1024,256]{1,0:T(8,128)(2,1)S(1)}, bf16[1024,1152]{1,0:...) custom-call(s32[8]{0:T(128)S(1)} %pad_add_fusion.refs_0_.table, ...), custom_call_target="tpu_custom_call" | custom-call | flops 4000000000 | tf_op jit(solution)/shard_map/pallas_call | solution.py:416
  52.8 1.3 collective-permute-start.5
  54.1 0.5 collective-permute-start.4
  54.6 0.1 collective-permute-start.3
  54.7 4.2 %shard_map.116.refs_7_ = bf16[1024,256]{1,0:T(8,128)(2,1)S(1)} custom-call(s32[8]{0:T(128)S(1)} %pad_add_fusion.refs_0_.table, bf16[4,1024,1024]{2,1,0:T(8,128)(2,1)S(1)} %get-tuple-element.20.e.refs_1_, f32[1024,128]{1,0:T(8,128)S(1)} %get-tuple-element.21.stat.refs_2_, bf16[1024,256]{1,0:T(8,128)(2,1)S(1)} %get-tuple-element.27.key, ...), custom_call_target="tpu_custom_call" | custom-call | flops 2000000000 | tf_op jit(solution)/shard_map/pallas_call | solution.py:456
  58.9 0.0 collective-permute-done.4.refs_3_
  59.0 6.0 %shard_map.117 = (f32[1024,1]{1,0:T(8,128)S(1)}, bf16[8,256,128]{2,1,0:T(8,128)(2,1)}) custom-call(s32[8]{0:T(128)S(1)} %pad_add_fusion.refs_0_.table, f32[1,1024]{1,0:T(1,128)S(1)} %get-tuple-element.24.refs_1_, f32[1,1024]{1,0:T(1,128)S(1)} %collective-permute-done.3.refs_2_, f32[1,1024]{1,0:T(1,128)S(1)} %collective-permute-done.4.refs_3_, ...), custom_call_target="tpu_custom_call" | custom-call | flops 2000000000 | tf_op jit(solution)/shard_map/pallas_call | solution.py:467
  64.9 8.2 %shard_map.118 = (bf16[272,1024]{1,0:T(8,128)(2,1)S(1)}, bf16[4,272,128]{2,1,0:T(8,128)(2,1)S(1)}, bf16[4,272,128]{2,1,0:T(8,128)(2,1)S(1)}) custom-call(s32[8]{0:T(128)S(1)} %pad_add_fusion.refs_0_.table, bf16[4,1024,1024]{2,1,0:T(8,128)(2,1)S(1)} %get-tuple-element.20.e.refs_1_, f32[1024,128]{1,0:T(8,128)S(1)} %get-tuple-element.21.stat.refs_2_, ...), custom_call_target="tpu_custom_call" | custom-call | flops 4000000000 | tf_op jit(solution)/shard_map/pallas_call | solution.py:482
  73.2 2.2 %collective-permute-start.15 = (bf16[4,272,128]{2,1,0:T(8,128)(2,1)S(1)}, bf16[4,272,128]{2,1,0:T(8,128)(2,1)}, u32[]{:S(2)}, u32[]{:S(2)}) collective-permute-start(bf16[4,272,128]{2,1,0:T(8,128)(2,1)S(1)} %get-tuple-element.33), channel_id=1, source_target_pairs={{0,4},{4,0},{8,12},{12,8},{16,20},{20,16},{24,28},{28,24},{1,5},{5... | collective-permute-start | bytes 835592 | tf_op jit(solution)/shard_map/ppermute | solution.py:510
  75.4 0.2 reduce.2
  75.6 0.8 fusion.7
  76.4 1.3 collective-permute-start.11
  77.6 0.5 collective-permute-start.10
  78.1 0.1 collective-permute-start.9
  78.2 3.7 %all-to-all-start.2 = ((bf16[8,256,128]{2,1,0:T(8,128)(2,1)}), bf16[8,256,128]{2,1,0:T(8,128)(2,1)S(1)}, u32[]{:S(2)}, u32[]{:S(2)}) async-start(bf16[8,256,128]{2,1,0:T(8,128)(2,1)} %get-tuple-element.31), calls=%async_computation.2 | async-start | bytes 1048576 | tf_op jit(solution)/shard_map/all_to_all | solution.py:375
  81.9 0.8 collective-permute-done.15
  82.7 1.0 add_convert_fusion
  83.8 1.2 collective-permute-start.16
  85.0 0.8 collective-permute-start.8
  85.9 0.9 collective-permute-start.7
  86.7 0.2 collective-permute-start.6
  87.0 3.7 %shard_map.119.refs_6_ = f32[256,1024]{1,0:T(8,128)S(1)} custom-call(s32[8]{0:T(128)S(1)} %pad_add_fusion.refs_0_.table, bf16[256,256]{1,0:T(8,128)(2,1)S(1)} %get-tuple-element.42.refs_1_, bf16[256,256]{1,0:T(8,128)(2,1)S(1)} %collective-permute-done.9.refs_2_, bf16[256,256]{1,0:T(8,128)(2,1)S(1)} %collective-permute-done.10.refs_3_, ...), custom_call_target="tpu_custom_call" | custom-call | flops 1000000000 | tf_op jit(solution)/shard_map/pallas_call | solution.py:519
  90.7 3.8 %collective-permute-done.16 = bf16[2,272,128]{2,1,0:T(8,128)(2,1)S(1)} collective-permute-done((bf16[2,272,128]{2,1,0:T(8,128)(2,1)S(1)}, bf16[2,272,128]{2,1,0:T(8,128)(2,1)S(1)}, u32[]{:S(2)}, u32[]{:S(2)}) %collective-permute-start.16) | collective-permute-done | bytes 139296 | tf_op jit(solution)/shard_map/ppermute | solution.py:510
  94.6 4.2 %collective-permute-start.17 = (bf16[1,272,128]{2,1,0:T(8,128)(2,1)S(1)}, bf16[1,272,128]{2,1,0:T(8,128)(2,1)S(1)}, u32[]{:S(2)}, u32[]{:S(2)}) collective-permute-start(bf16[1,272,128]{2,1,0:T(8,128)(2,1)S(1)} %slice_bitcast_fusion.2), channel_id=1, source_target_pairs={{0,16},{4,20},{8,24},{12,28},{16,0},{20,4},{24,8},{28,12},{1,17},{... | collective-permute-start | bytes 208904 | tf_op jit(solution)/shard_map/ppermute | solution.py:510
  98.8 5.1 %shard_map.120 = bf16[8,32,1024]{2,1,0:T(8,128)(2,1)} custom-call(s32[8]{0:T(128)S(1)} %pad_add_fusion.refs_0_.table, bf16[272,256]{1,0:T(8,128)(2,1)S(1)} %get-tuple-element.38.refs_1_, bf16[272,256]{1,0:T(8,128)(2,1)S(1)} %collective-permute-done.6.refs_2_, bf16[272,256]{1,0:T(8,128)(2,1)S(1)} %collective-permute-done.7.refs_3_, ...), custom_call_target="tpu_custom_call" | custom-call | flops 1000000000 | tf_op jit(solution)/shard_map/pallas_call | solution.py:528
  103.9 1.6 %collective-permute-start.19 = (bf16[272,128]{1,0:T(8,128)(2,1)S(1)}, bf16[272,128]{1,0:T(8,128)(2,1)S(1)}, u32[]{:S(2)}, u32[]{:S(2)}) collective-permute-start(bf16[272,128]{1,0:T(8,128)(2,1)S(1)} %bitcast.78), channel_id=1, source_target_pairs={{0,2},{1,3},{2,0},{3,1},{4,6},{5,7},{6,4},{7,5},{8,10},{9,11},{10,... | collective-permute-start | bytes 208904 | tf_op jit(solution)/shard_map/ppermute | solution.py:372
  105.5 3.5 %all-to-all-start.1 = ((bf16[8,32,1024]{2,1,0:T(8,128)(2,1)}), bf16[8,32,1024]{2,1,0:T(8,128)(2,1)S(1)}, u32[]{:S(2)}, u32[]{:S(2)}) async-start(bf16[8,32,1024]{2,1,0:T(8,128)(2,1)} %shard_map.120), calls=%async_computation.1 | async-start | bytes 1048576 | tf_op jit(solution)/shard_map/all_to_all | solution.py:375
  109.0 0.1 collective-permute-start.18
  109.1 0.5 collective-permute-start.20
  109.6 0.1 reduce_sum.12
  109.7 0.6 collective-permute-start.13
  110.3 3.7 %collective-permute-done.13 = bf16[256,128]{1,0:T(8,128)(2,1)S(1)} collective-permute-done((bf16[256,128]{1,0:T(8,128)(2,1)S(1)}, bf16[256,128]{1,0:T(8,128)(2,1)S(1)}, u32[]{:S(2)}, u32[]{:S(2)}) %collective-permute-start.13) | collective-permute-done | bytes 65568 | tf_op jit(solution)/shard_map/ppermute | solution.py:372
  114.1 0.6 gather_fusion.2
  114.7 0.2 fusion
  115.0 0.3 collective-permute-done.14
  115.3 0.0 copy-start.8
  115.3 0.6 gather_fusion.1
  115.9 0.1 pad_maximum_fusion
  116.0 0.7 dynamic-slice_bitcast_fusion
  116.7 6.0 %all-to-all-done.1 = bf16[8,32,1024]{2,1,0:T(8,128)(2,1)S(1)} async-done(((bf16[8,32,1024]{2,1,0:T(8,128)(2,1)}), bf16[8,32,1024]{2,1,0:T(8,128)(2,1)S(1)}, u32[]{:S(2)}, u32[]{:S(2)}) %all-to-all-start.1) | async-done | bytes 524320 | tf_op jit(solution)/shard_map/all_to_all | solution.py:375
  122.7 3.6 %all-to-all-start.3 = ((bf16[8,96,128]{2,1,0:T(8,128)(2,1)}), bf16[8,96,128]{2,1,0:T(8,128)(2,1)S(1)}, u32[]{:S(2)}, u32[]{:S(2)}) async-start(bf16[8,96,128]{2,1,0:T(8,128)(2,1)} %dynamic-slice_bitcast_fusion), calls=%async_computation.3 | async-start | bytes 393216 | tf_op jit(solution)/shard_map/all_to_all | solution.py:375
  126.3 0.1 dynamic_slice.13
  126.4 0.7 broadcast_multiply_fusion
  127.2 1.4 %gather_fusion = bf16[8,32,1024]{2,1,0:T(8,128)(2,1)} fusion(bf16[8,32,1024]{2,1,0:T(8,128)(2,1)S(1)} %all-to-all-done.1, s32[1024]{0:T(1024)S(1)} %pad_clamp_fusion.1), kind=kCustom, calls=%fused_computation | custom fusion | bytes 1048608 | tf_op jit(solution)/shard_map/gather | solution.py:551
  128.6 5.5 %all-to-all-done.3 = bf16[8,96,128]{2,1,0:T(8,128)(2,1)S(1)} async-done(((bf16[8,96,128]{2,1,0:T(8,128)(2,1)}), bf16[8,96,128]{2,1,0:T(8,128)(2,1)S(1)}, u32[]{:S(2)}, u32[]{:S(2)}) %all-to-all-start.3) | async-done | bytes 196640 | tf_op jit(solution)/shard_map/all_to_all | solution.py:375
  134.1 0.8 copy_bitcast_fusion
  (46 shorter events, 0.3 us)
Async XLA Ops:
  0.6 10.1 %copy-start = (s32[8,3]{0,1:T(4,128)S(1)}, s32[8,3]{0,1:T(4,128)}, u32[]{:S(2)}) copy-start(s32[8,3]{0,1:T(4,128)} %param.13) | copy-start | bytes 292
  0.6 10.5 %copy-start.4 = (f32[1024]{0:T(1024)S(1)}, f32[1024]{0:T(1024)}, u32[]{:S(2)}) copy-start(f32[1024]{0:T(1024)} %param.17) | copy-start | bytes 12292
  0.7 10.5 %copy-start.1 = (bf16[1024,1024]{1,0:T(8,128)(2,1)S(1)}, bf16[1024,1024]{1,0:T(8,128)(2,1)}, u32[]{:S(2)}) copy-start(bf16[1024,1024]{1,0:T(8,128)(2,1)} %w_out.1) | copy-start | bytes 6291460
  0.7 0.8 copy-start.7
  3.5 23.2 %all-to-all-start = ((bf16[8,32,1152]{2,1,0:T(8,128)(2,1)}), bf16[8,32,1152]{2,1,0:T(8,128)(2,1)S(1)}, u32[]{:S(2)}, u32[]{:S(2)}) async-start(bf16[8,32,1152]{2,1,0:T(8,128)(2,1)} %shard_map.112), calls=%async_computation | async-start | bytes 1179648 | tf_op jit(solution)/shard_map/all_to_all | solution.py:375
  11.1 15.5 %copy-start.5 = (f32[1024]{0:T(1024)S(1)}, f32[1024]{0:T(1024)}, u32[]{:S(2)}) copy-start(f32[1024]{0:T(1024)} %param.14) | copy-start | bytes 12292
  11.1 15.5 %copy-start.6 = (s32[1,8]{1,0:T(1,128)S(1)}, s32[1,8]{1,0:T(1,128)}, u32[]{:S(2)}) copy-start(s32[1,8]{1,0:T(1,128)} %refs_8_.1) | copy-start | bytes 100
  14.0 0.7 copy-start.2
  27.5 13.7 %collective-permute-start.1 = (bf16[256,1152]{1,0:T(8,128)(2,1)S(1)}, bf16[256,1152]{1,0:T(8,128)(2,1)S(1)}, u32[]{:S(2)}, u32[]{:S(2)}) collective-permute-start(bf16[256,1152]{1,0:T(8,128)(2,1)S(1)} %bitcast.62), channel_id=1, source_target_pairs={{0,2},{1,3},{2,0},{3,1},{4,6},{5,7},{6,4},{7,5},{8,10},{9,11},{10,... | collective-permute-start | bytes 1769480 | tf_op jit(solution)/shard_map/ppermute | solution.py:372
  29.1 12.1 %collective-permute-start = (bf16[256,1152]{1,0:T(8,128)(2,1)S(1)}, bf16[256,1152]{1,0:T(8,128)(2,1)S(1)}, u32[]{:S(2)}, u32[]{:S(2)}) collective-permute-start(bf16[256,1152]{1,0:T(8,128)(2,1)S(1)} %bitcast.63), channel_id=1, source_target_pairs={{0,1},{1,0},{2,3},{3,2},{4,5},{5,4},{6,7},{7,6},{8,9},{9,8},{10,11... | collective-permute-start | bytes 1769480 | tf_op jit(solution)/shard_map/ppermute | solution.py:372
  41.2 2.0 %collective-permute-start.2 = (bf16[256,1152]{1,0:T(8,128)(2,1)S(1)}, bf16[256,1152]{1,0:T(8,128)(2,1)S(1)}, u32[]{:S(2)}, u32[]{:S(2)}) collective-permute-start(bf16[256,1152]{1,0:T(8,128)(2,1)S(1)} %collective-permute-done.1.refs_3_), channel_id=1, source_target_pairs={{0,1},{1,0},{2,3},{3,2},{4,5},{5,4},{6,7},{7,6},{8,9},{9,8},{10,11... | collective-permute-start | bytes 1769480 | tf_op jit(solution)/shard_map/ppermute | solution.py:372
  52.8 6.1 %collective-permute-start.5 = (f32[1,1024]{1,0:T(1,128)S(1)}, f32[1,1024]{1,0:T(1,128)S(1)}, u32[]{:S(2)}, u32[]{:S(2)}) collective-permute-start(f32[1,1024]{1,0:T(1,128)S(1)} %get-tuple-element.24.refs_1_), channel_id=1, source_target_pairs={{0,3},{1,2},{2,1},{3,0},{4,7},{5,6},{6,5},{7,4},{8,11},{9,10},{10,... | collective-permute-start | bytes 12296 | tf_op jit(solution)/shard_map/ppermute | solution.py:372
  54.1 4.8 %collective-permute-start.4 = (f32[1,1024]{1,0:T(1,128)S(1)}, f32[1,1024]{1,0:T(1,128)S(1)}, u32[]{:S(2)}, u32[]{:S(2)}) collective-permute-start(f32[1,1024]{1,0:T(1,128)S(1)} %get-tuple-element.24.refs_1_), channel_id=1, source_target_pairs={{0,2},{1,3},{2,0},{3,1},{4,6},{5,7},{6,4},{7,5},{8,10},{9,11},{10,... | collective-permute-start | bytes 12296 | tf_op jit(solution)/shard_map/ppermute | solution.py:372
  54.6 4.3 %collective-permute-start.3 = (f32[1,1024]{1,0:T(1,128)S(1)}, f32[1,1024]{1,0:T(1,128)S(1)}, u32[]{:S(2)}, u32[]{:S(2)}) collective-permute-start(f32[1,1024]{1,0:T(1,128)S(1)} %get-tuple-element.24.refs_1_), channel_id=1, source_target_pairs={{0,1},{1,0},{2,3},{3,2},{4,5},{5,4},{6,7},{7,6},{8,9},{9,8},{10,11... | collective-permute-start | bytes 12296 | tf_op jit(solution)/shard_map/ppermute | solution.py:372
  73.2 9.6 %collective-permute-start.15 = (bf16[4,272,128]{2,1,0:T(8,128)(2,1)S(1)}, bf16[4,272,128]{2,1,0:T(8,128)(2,1)}, u32[]{:S(2)}, u32[]{:S(2)}) collective-permute-start(bf16[4,272,128]{2,1,0:T(8,128)(2,1)S(1)} %get-tuple-element.33), channel_id=1, source_target_pairs={{0,4},{4,0},{8,12},{12,8},{16,20},{20,16},{24,28},{28,24},{1,5},{5... | collective-permute-start | bytes 835592 | tf_op jit(solution)/shard_map/ppermute | solution.py:510
  76.4 9.5 %collective-permute-start.11 = (bf16[256,256]{1,0:T(8,128)(2,1)}, bf16[256,256]{1,0:T(8,128)(2,1)S(1)}, u32[]{:S(2)}, u32[]{:S(2)}) collective-permute-start(bf16[256,256]{1,0:T(8,128)(2,1)} %get-tuple-element.39), channel_id=1, source_target_pairs={{0,3},{1,2},{2,1},{3,0},{4,7},{5,6},{6,5},{7,4},{8,11},{9,10},{10,... | collective-permute-start | bytes 393224 | tf_op jit(solution)/shard_map/ppermute | solution.py:372
  77.6 9.1 %collective-permute-start.10 = (bf16[256,256]{1,0:T(8,128)(2,1)}, bf16[256,256]{1,0:T(8,128)(2,1)S(1)}, u32[]{:S(2)}, u32[]{:S(2)}) collective-permute-start(bf16[256,256]{1,0:T(8,128)(2,1)} %get-tuple-element.40), channel_id=1, source_target_pairs={{0,2},{1,3},{2,0},{3,1},{4,6},{5,7},{6,4},{7,5},{8,10},{9,11},{10,... | collective-permute-start | bytes 393224 | tf_op jit(solution)/shard_map/ppermute | solution.py:372
  78.1 8.9 %collective-permute-start.9 = (bf16[256,256]{1,0:T(8,128)(2,1)}, bf16[256,256]{1,0:T(8,128)(2,1)S(1)}, u32[]{:S(2)}, u32[]{:S(2)}) collective-permute-start(bf16[256,256]{1,0:T(8,128)(2,1)} %get-tuple-element.41), channel_id=1, source_target_pairs={{0,1},{1,0},{2,3},{3,2},{4,5},{5,4},{6,7},{7,6},{8,9},{9,8},{10,11... | collective-permute-start | bytes 393224 | tf_op jit(solution)/shard_map/ppermute | solution.py:372
  78.2 27.3 %all-to-all-start.2 = ((bf16[8,256,128]{2,1,0:T(8,128)(2,1)}), bf16[8,256,128]{2,1,0:T(8,128)(2,1)S(1)}, u32[]{:S(2)}, u32[]{:S(2)}) async-start(bf16[8,256,128]{2,1,0:T(8,128)(2,1)} %get-tuple-element.31), calls=%async_computation.2 | async-start | bytes 1048576 | tf_op jit(solution)/shard_map/all_to_all | solution.py:375
  83.8 10.7 %collective-permute-start.16 = (bf16[2,272,128]{2,1,0:T(8,128)(2,1)S(1)}, bf16[2,272,128]{2,1,0:T(8,128)(2,1)S(1)}, u32[]{:S(2)}, u32[]{:S(2)}) collective-permute-start(bf16[2,272,128]{2,1,0:T(8,128)(2,1)S(1)} %slice_bitcast_fusion), channel_id=1, source_target_pairs={{0,8},{4,12},{8,0},{12,4},{16,24},{20,28},{24,16},{28,20},{1,9},{5... | collective-permute-start | bytes 417800 | tf_op jit(solution)/shard_map/ppermute | solution.py:510
  85.0 13.7 %collective-permute-start.8 = (bf16[272,256]{1,0:T(8,128)(2,1)S(1)}, bf16[272,256]{1,0:T(8,128)(2,1)S(1)}, u32[]{:S(2)}, u32[]{:S(2)}) collective-permute-start(bf16[272,256]{1,0:T(8,128)(2,1)S(1)} %get-tuple-element.35), channel_id=1, source_target_pairs={{0,3},{1,2},{2,1},{3,0},{4,7},{5,6},{6,5},{7,4},{8,11},{9,10},{10,... | collective-permute-start | bytes 417800 | tf_op jit(solution)/shard_map/ppermute | solution.py:372
  85.9 12.9 %collective-permute-start.7 = (bf16[272,256]{1,0:T(8,128)(2,1)S(1)}, bf16[272,256]{1,0:T(8,128)(2,1)S(1)}, u32[]{:S(2)}, u32[]{:S(2)}) collective-permute-start(bf16[272,256]{1,0:T(8,128)(2,1)S(1)} %get-tuple-element.36), channel_id=1, source_target_pairs={{0,2},{1,3},{2,0},{3,1},{4,6},{5,7},{6,4},{7,5},{8,10},{9,11},{10,... | collective-permute-start | bytes 417800 | tf_op jit(solution)/shard_map/ppermute | solution.py:372
  86.7 12.0 %collective-permute-start.6 = (bf16[272,256]{1,0:T(8,128)(2,1)S(1)}, bf16[272,256]{1,0:T(8,128)(2,1)S(1)}, u32[]{:S(2)}, u32[]{:S(2)}) collective-permute-start(bf16[272,256]{1,0:T(8,128)(2,1)S(1)} %get-tuple-element.37), channel_id=1, source_target_pairs={{0,1},{1,0},{2,3},{3,2},{4,5},{5,4},{6,7},{7,6},{8,9},{9,8},{10,11... | collective-permute-start | bytes 417800 | tf_op jit(solution)/shard_map/ppermute | solution.py:372
  87.0 11.8 %copy-start.3 = (bf16[48,1024]{1,0:T(8,128)(2,1)S(1)}, bf16[48,1024]{1,0:T(8,128)(2,1)}, u32[]{:S(2)}) copy-start(bf16[48,1024]{1,0:T(8,128)(2,1)} %copy-done.2) | copy-start | bytes 294916
  94.6 9.3 %collective-permute-start.17 = (bf16[1,272,128]{2,1,0:T(8,128)(2,1)S(1)}, bf16[1,272,128]{2,1,0:T(8,128)(2,1)S(1)}, u32[]{:S(2)}, u32[]{:S(2)}) collective-permute-start(bf16[1,272,128]{2,1,0:T(8,128)(2,1)S(1)} %slice_bitcast_fusion.2), channel_id=1, source_target_pairs={{0,16},{4,20},{8,24},{12,28},{16,0},{20,4},{24,8},{28,12},{1,17},{... | collective-permute-start | bytes 208904 | tf_op jit(solution)/shard_map/ppermute | solution.py:510
  103.9 5.2 %collective-permute-start.19 = (bf16[272,128]{1,0:T(8,128)(2,1)S(1)}, bf16[272,128]{1,0:T(8,128)(2,1)S(1)}, u32[]{:S(2)}, u32[]{:S(2)}) collective-permute-start(bf16[272,128]{1,0:T(8,128)(2,1)S(1)} %bitcast.78), channel_id=1, source_target_pairs={{0,2},{1,3},{2,0},{3,1},{4,6},{5,7},{6,4},{7,5},{8,10},{9,11},{10,... | collective-permute-start | bytes 208904 | tf_op jit(solution)/shard_map/ppermute | solution.py:372
  105.5 17.2 %all-to-all-start.1 = ((bf16[8,32,1024]{2,1,0:T(8,128)(2,1)}), bf16[8,32,1024]{2,1,0:T(8,128)(2,1)S(1)}, u32[]{:S(2)}, u32[]{:S(2)}) async-start(bf16[8,32,1024]{2,1,0:T(8,128)(2,1)} %shard_map.120), calls=%async_computation.1 | async-start | bytes 1048576 | tf_op jit(solution)/shard_map/all_to_all | solution.py:375
  109.0 5.0 %collective-permute-start.18 = (bf16[272,128]{1,0:T(8,128)(2,1)S(1)}, bf16[272,128]{1,0:T(8,128)(2,1)S(1)}, u32[]{:S(2)}, u32[]{:S(2)}) collective-permute-start(bf16[272,128]{1,0:T(8,128)(2,1)S(1)} %bitcast.79), channel_id=1, source_target_pairs={{0,1},{1,0},{2,3},{3,2},{4,5},{5,4},{6,7},{7,6},{8,9},{9,8},{10,11... | collective-permute-start | bytes 208904 | tf_op jit(solution)/shard_map/ppermute | solution.py:372
  109.1 4.9 %collective-permute-start.20 = (bf16[272,128]{1,0:T(8,128)(2,1)S(1)}, bf16[272,128]{1,0:T(8,128)(2,1)S(1)}, u32[]{:S(2)}, u32[]{:S(2)}) collective-permute-start(bf16[272,128]{1,0:T(8,128)(2,1)S(1)} %collective-permute-done.19), channel_id=1, source_target_pairs={{0,1},{1,0},{2,3},{3,2},{4,5},{5,4},{6,7},{7,6},{8,9},{9,8},{10,11... | collective-permute-start | bytes 208904 | tf_op jit(solution)/shard_map/ppermute | solution.py:372
  109.7 4.3 %collective-permute-start.13 = (bf16[256,128]{1,0:T(8,128)(2,1)S(1)}, bf16[256,128]{1,0:T(8,128)(2,1)S(1)}, u32[]{:S(2)}, u32[]{:S(2)}) collective-permute-start(bf16[256,128]{1,0:T(8,128)(2,1)S(1)} %reduce_sum.12), channel_id=1, source_target_pairs={{0,2},{1,3},{2,0},{3,1},{4,6},{5,7},{6,4},{7,5},{8,10},{9,11},{10,... | collective-permute-start | bytes 196616 | tf_op jit(solution)/shard_map/ppermute | solution.py:372
  110.3 4.7 %collective-permute-start.12 = (bf16[256,128]{1,0:T(8,128)(2,1)S(1)}, bf16[256,128]{1,0:T(8,128)(2,1)S(1)}, u32[]{:S(2)}, u32[]{:S(2)}) collective-permute-start(bf16[256,128]{1,0:T(8,128)(2,1)S(1)} %reduce_sum.12), channel_id=1, source_target_pairs={{0,1},{1,0},{2,3},{3,2},{4,5},{5,4},{6,7},{7,6},{8,9},{9,8},{10,11... | collective-permute-start | bytes 196616 | tf_op jit(solution)/shard_map/ppermute | solution.py:372
  114.0 1.3 collective-permute-start.14
  115.3 11.0 %copy-start.8 = (s32[1,8]{1,0:T(1,128)S(1)}, s32[1,8]{1,0:T(1,128)}, u32[]{:S(2)}) copy-start(s32[1,8]{1,0:T(1,128)} %dest.1) | copy-start | bytes 100
  122.7 11.4 %all-to-all-start.3 = ((bf16[8,96,128]{2,1,0:T(8,128)(2,1)}), bf16[8,96,128]{2,1,0:T(8,128)(2,1)S(1)}, u32[]{:S(2)}, u32[]{:S(2)}) async-start(bf16[8,96,128]{2,1,0:T(8,128)(2,1)} %dynamic-slice_bitcast_fusion), calls=%async_computation.3 | async-start | bytes 393216 | tf_op jit(solution)/shard_map/all_to_all | solution.py:375
